TPU v7x, 32 devices: a whole 2x2x4 slice. The times are simulated.
32 devices in a mesh: dp: 4 (over y, x), expert: 8 (over z, core).
Axes of the slice: x: 2, y: 2, z: 4, core: 2. Of those that a mesh axis runs over, the one named last changes fastest.
Arguments:
- tokens: bfloat16 [10240, 2048], P(('dp', 'expert')), may hold values from -6 to 6
- out_grad: bfloat16 [10240, 2048], P(('dp', 'expert')), may hold values from -6 to 6
- expert_ids: int32 [10240, 2], P(('dp', 'expert')), may hold values from 0 to 7, all different within a row; in each aligned block of 320 rows (0 to 319, 320 to 639, ...) at most 120 rows name the same one
- route_weight: bfloat16 [10240, 2], P(('dp', 'expert')), may hold values from 0.099609375 to 1
- w_gate: bfloat16 [8, 2048, 768], P('expert', 'dp'), may hold values from -0.125 to 0.125
- w_up: bfloat16 [8, 2048, 768], P('expert', 'dp'), may hold values from -0.125 to 0.125
- w_down: bfloat16 [8, 768, 2048], P('expert', None, 'dp'), may hold values from -0.21875 to 0.21875
Outputs:
- token_grad: bfloat16 [10240, 2048], P(('dp', 'expert'))
- route_grad: bfloat16 [10240, 2], P(('dp', 'expert'))
- gate_grad: bfloat16 [8, 2048, 768], P('expert', 'dp')
- up_grad: bfloat16 [8, 2048, 768], P('expert', 'dp')
- down_grad: bfloat16 [8, 768, 2048], P('expert', None, 'dp')
Inputs may be any that keep to these rules, and one draw needn't show every extreme that they name: `expert_ids`: each row names 2 different experts. In the rows of one device no expert is named more than 120 times, a bound that some block reaches in some device.
All inputs are finite; a program needn't handle non-finite values.
Results may differ from a plain program's by a relative error of at most 0.014.
Values may be sent and summed in bfloat16 or wider, within the bound.
A program may use at most 128 MiB of HBM per device.

v0:
```python
import functools
import jax
import jax.numpy as jnp
from jax import lax
from jax.experimental import pallas as pl
from jax.experimental.pallas import tpu as pltpu
from jax.sharding import PartitionSpec as P


MESH = pl.DeviceIdType.MESH
BF16 = jnp.bfloat16
F32 = jnp.float32


def dot(left, right, over_left=1, over_right=0):
    return lax.dot_general(
        left, right, (((over_left,), (over_right,)), ((), ())), preferred_element_type=F32
    )


class Chain:
    def __init__(self):
        self.g = lax.axis_index("dp")
        self.me = lax.axis_index("expert")
        self.c = self.me % 2
        self.z = self.me // 2
        self.half = self.z // 2
        self.far = 1 - self.half
        self.is_mid = (self.z + self.half) % 2 == 1
        self.is_end = (self.z + self.half) % 2 == 0
        self.z_mid = 1 + self.half
        self.z_end = 3 * self.half
        self.z_far_mid = 1 + self.far
        self.z_far_end = 3 * self.far
        self.z_near = self.z_mid + self.z_end - self.z

    def at(self, z, c):
        return (self.g, 2 * z + c)


def greet(chain, ranks, groups):
    barrier = pltpu.get_barrier_semaphore()
    for step in range(1, ranks):
        pl.semaphore_signal(
            barrier, inc=1, device_id=(chain.g, (chain.me + step) % ranks), device_id_type=MESH
        )
    for step in range(1, groups):
        pl.semaphore_signal(
            barrier, inc=1, device_id=((chain.g + step) % groups, chain.me), device_id_type=MESH
        )
    pl.semaphore_wait(barrier, ranks + groups - 2)


def neighbours(g):
    along_x = g + 1 - 2 * (g % 2)
    along_y = (g + 2) % 4
    return along_x, along_y


def send(src, dst, send_sem, recv_sem, device):
    return pltpu.make_async_remote_copy(
        src_ref=src, dst_ref=dst, send_sem=send_sem, recv_sem=recv_sem,
        device_id=device, device_id_type=MESH,
    )


def forward_kernel(
    cap,
    ids_ref, weight_ref, tokens_ref, grads_ref, wg_ref, wu_ref, wd_ref,
    full_gate_out, full_up_out, rows_out, hidden_out, gate_delta_out, up_delta_out, dots_out, table_out,
    raw, rows, stage_d, stage_e, full_gate, full_up, full_down, gate_val, up_val, hg_val, select,
    load_sem, raw_ss, raw_rs, e_ss, e_rs, d_ss, d_rs, tab_ss, tab_rs,
    w_ls, wa_ss, wa_rs, wf_ss, wf_rs, out_sem,
):
    chain = Chain()
    g, me, c, z = chain.g, chain.me, chain.c, chain.z
    is_mid, is_end = chain.is_mid, chain.is_end
    groups = lax.axis_size("dp")
    ranks = lax.axis_size("expert")
    steps = 2 * groups
    width = raw.shape[-1]
    count = raw.shape[2]
    slot_rows = rows.shape[2]
    along_x, along_y = neighbours(g)
    fulls = (full_gate, full_up, full_down)
    shards = (wg_ref, wu_ref, wd_ref)

    def load(k):
        source = tokens_ref if k < groups else grads_ref
        return pltpu.make_async_copy(
            source.at[:, pl.ds((k % groups) * width, width)], raw.at[0, k], load_sem.at[k]
        )

    for k in range(steps):
        load(k).start()
    for w in range(3):
        pltpu.make_async_copy(shards[w].at[0], fulls[w].at[g], w_ls.at[w]).start()

    greet(chain, ranks, groups)

    def shard_to(w, way):
        device = (along_x, me) if way == 0 else (along_y, me)
        return send(shards[w].at[0], fulls[w].at[g], wa_ss.at[w, way], wa_rs.at[w, way], device)

    def forward_half(w, way):
        owner = along_y if way == 0 else along_x
        device = (along_x, me) if way == 0 else (along_y, me)
        half = fulls[w].shape[1] // 2
        piece = fulls[w].at[owner, pl.ds(way * half, half)]
        return send(piece, piece, wf_ss.at[w, way], wf_rs.at[w, way], device)

    for w in range(3):
        for way in range(2):
            shard_to(w, way).start()

    experts = lax.broadcasted_iota(jnp.int32, (ranks, count), 0)
    named = [experts == ids_ref[k : k + 1, :] for k in range(ids_ref.shape[0])]
    hits = functools.reduce(jnp.logical_or, named)
    before = lax.broadcasted_iota(jnp.int32, (count, count), 0) < lax.broadcasted_iota(
        jnp.int32, (count, count), 1
    )
    order = dot(hits.astype(F32).astype(BF16), before.astype(F32).astype(BF16))
    table_out[0, 0:ranks, :] = jnp.where(hits, order, -1.0)
    weight = jnp.zeros((ranks, count), F32)
    for k in range(ids_ref.shape[0]):
        weight = jnp.where(named[k], weight_ref[k : k + 1, :], weight)
    table_out[0, ranks : 2 * ranks, :] = weight

    rows[:, :, cap:, :] = jnp.zeros((steps, ranks, slot_rows - cap, width), BF16)

    def table_send(slot, sem, zz):
        return send(
            table_out.at[0], table_out.at[slot], tab_ss.at[sem], tab_rs.at[slot - 1], chain.at(zz, c)
        )

    @pl.when(is_end)
    def _():
        table_send(1, 0, chain.z_mid).start()
        table_send(3, 1, chain.z_far_mid).start()

    @pl.when(is_mid)
    def _():
        table_send(2, 0, chain.z_far_mid).start()

    targets = (me, me + 1 - 2 * c, 2 * chain.z_near, 2 * chain.z_near + 1)

    def selectors(j):
        slots = lax.broadcasted_iota(jnp.int32, (slot_rows, count), 0).astype(F32)
        for i, rank in enumerate(targets):
            hit = table_out[j, pl.ds(rank, 1), :] == slots
            block = pl.ds(i * slot_rows, slot_rows)
            select[0, j, block, :] = jnp.where(hit, 1.0, 0.0).astype(BF16)
            select[1, j, block, :] = jnp.where(
                hit, table_out[j, pl.ds(ranks + rank, 1), :], 0.0
            ).astype(BF16)

    selectors(0)

    def gather(j, k, z_from, blocks, e_slot):
        picked = dot(select[k // groups, j, 0 : blocks * slot_rows, :], raw[j, k]).astype(BF16)
        parts = [picked[i * slot_rows : (i + 1) * slot_rows] for i in range(blocks)]
        rows[k, 4 * c + z_from] = parts[0]
        stage_d[k, z_from] = parts[1]
        for i in range(2, blocks):
            stage_e[k, i - 2, e_slot] = parts[i]

    full = pl.ds(0, cap)

    def own_raw(k):
        return send(raw.at[0, k], raw.at[2, k], raw_ss.at[0, k], raw_rs.at[1, k], chain.at(chain.z_far_mid, c))

    def end_raw(k):
        return send(raw.at[0, k], raw.at[1, k], raw_ss.at[0, k], raw_rs.at[0, k], chain.at(chain.z_mid, c))

    def onward_raw(k):
        return send(raw.at[1, k], raw.at[3, k], raw_ss.at[1, k], raw_rs.at[2, k], chain.at(chain.z_far_mid, c))

    def own_to_end(k, i):
        return send(
            stage_e.at[k, i, 0, full], rows.at[k, 4 * c + z, full],
            e_ss.at[k, 0, i], e_rs.at[k, 0, c], chain.at(chain.z_end, i),
        )

    def far_to_end(k, i):
        return send(
            stage_e.at[k, i, pl.ds(1, 2), full], rows.at[k, pl.ds(4 * c + 2 * chain.far, 2), full],
            e_ss.at[k, 1, i], e_rs.at[k, 1, c], chain.at(chain.z_end, i),
        )

    def mid_to_partner(k):
        return send(
            stage_d.at[k, :, full], rows.at[k, pl.ds(4 * c, 4), full], d_ss.at[k], d_rs.at[k], chain.at(z, 1 - c)
        )

    def end_to_partner(k):
        return send(
            stage_d.at[k, z, full], rows.at[k, 4 * c + z, full], d_ss.at[k], d_rs.at[k], chain.at(z, 1 - c)
        )

    def own_block_from(k, core):
        return send(
            stage_e.at[k, 0, 0, full], rows.at[k, 4 * core + chain.z_mid, full],
            e_ss.at[k, 0, 0], e_rs.at[k, 0, core], chain.at(chain.z_mid, core),
        )

    def far_blocks_from(k, core):
        return send(
            stage_e.at[k, 0, pl.ds(1, 2), full], rows.at[k, pl.ds(4 * core + 2 * chain.far, 2), full],
            e_ss.at[k, 1, 0], e_rs.at[k, 1, core], chain.at(chain.z_mid, core),
        )

    def landed(k):
        @pl.when(is_mid)
        def _():
            mid_to_partner(k).wait_recv()

        @pl.when(is_end)
        def _():
            end_to_partner(k).wait_recv()
            for core in range(2):
                own_block_from(k, core).wait_recv()
                far_blocks_from(k, core).wait_recv()

    def load_wait(k):
        pltpu.make_async_copy(
            tokens_ref.at[:, pl.ds(0, width)], raw.at[0, k], load_sem.at[k]
        ).wait()

    def step(k, carry):
        @pl.when(is_mid & (k < steps))
        def _():
            load_wait(k)
            own_raw(k).start()
            gather(0, k, z, 4, 0)
            own_to_end(k, 0).start()
            own_to_end(k, 1).start()

            @pl.when(k == 0)
            def _():
                table_send(1, 0, chain.z_mid).wait_recv()
                selectors(1)

            end_raw(k).wait_recv()
            onward_raw(k).start()
            gather(1, k, chain.z_end, 2, 0)

        @pl.when(is_mid & (k >= 1))
        def _():
            @pl.when(k == 1)
            def _():
                table_send(2, 0, chain.z_far_mid).wait_recv()
                table_send(3, 0, chain.z_far_mid).wait_recv()
                selectors(2)
                selectors(3)

            j = k - 1
            own_raw(j).wait_recv()
            gather(2, j, chain.z_far_mid, 4, 1 + chain.half)
            onward_raw(j).wait_recv()
            gather(3, j, chain.z_far_end, 4, 1 + chain.far)
            far_to_end(j, 0).start()
            far_to_end(j, 1).start()
            mid_to_partner(j).start()

        @pl.when(is_end & (k < steps))
        def _():
            load_wait(k)
            end_raw(k).start()
            gather(0, k, z, 2, 0)
            end_to_partner(k).start()

        for w in range(3):
            @pl.when(k == w + 1)
            def _():
                for way in range(2):
                    shard_to(w, 1 - way).wait_recv()
                    forward_half(w, way).start()

        @pl.when(k == groups + 1)
        def _():
            for kk in range(groups):
                landed(kk)
            for w in range(2):
                pltpu.make_async_copy(shards[w].at[0], fulls[w].at[g], w_ls.at[w]).wait()
                for way in range(2):
                    forward_half(w, way).wait_recv()

        @pl.when(k >= groups + 1)
        def _():
            b = 2 * (k - groups - 1)
            for half in range(2):
                block = b + half
                piece = [rows[kk, block] for kk in range(groups)]
                gate = functools.reduce(jnp.add, [dot(piece[kk], full_gate[kk]) for kk in range(groups)])
                up = functools.reduce(jnp.add, [dot(piece[kk], full_up[kk]) for kk in range(groups)])
                gate_val[block] = gate
                up_val[block] = up
                hidden_out[block] = (gate * jax.nn.sigmoid(gate) * up).astype(BF16)

        return carry

    lax.fori_loop(0, steps + 1, step, 0)

    outs = [
        pltpu.make_async_copy(full_gate, full_gate_out, out_sem.at[0]),
        pltpu.make_async_copy(full_up, full_up_out, out_sem.at[1]),
    ]
    for copy in outs:
        copy.start()
    first = pltpu.make_async_copy(rows.at[pl.ds(0, groups)], rows_out.at[pl.ds(0, groups)], out_sem.at[2])
    first.start()

    pltpu.make_async_copy(shards[2].at[0], fulls[2].at[g], w_ls.at[2]).wait()
    for way in range(2):
        forward_half(2, way).wait_recv()

    def hidden_grad(q, carry):
        landed(groups + q)
        pltpu.make_async_copy(rows.at[groups + q], rows_out.at[groups + q], out_sem.at[3 + q]).start()

        def tile(t, carry):
            value = dot(rows[groups + q, t], full_down[q], 1, 1)

            @pl.when(q == 0)
            def _():
                hg_val[t] = value

            @pl.when(q > 0)
            def _():
                hg_val[t] += value

            return carry

        return lax.fori_loop(0, ranks, tile, carry)

    lax.fori_loop(0, groups, hidden_grad, 0)

    def deltas(t, carry):
        gate, up, grad = gate_val[t], up_val[t], hg_val[t]
        sig = jax.nn.sigmoid(gate)
        gate_delta_out[t] = (grad * up * sig * (1.0 + gate * (1.0 - sig))).astype(BF16)
        up_delta_out[t] = (grad * (gate * sig)).astype(BF16)
        dots_out[t] = jnp.broadcast_to(
            jnp.sum(hidden_out[t].astype(F32) * grad, axis=1, keepdims=True), dots_out.shape[1:]
        )
        return carry

    lax.fori_loop(0, ranks, deltas, 0)

    for copy in outs:
        copy.wait()
    first.wait()
    for q in range(groups):
        pltpu.make_async_copy(rows.at[groups + q], rows_out.at[groups + q], out_sem.at[3 + q]).wait()
    for w in range(3):
        for way in range(2):
            shard_to(w, way).wait_send()
            forward_half(w, way).wait_send()

    def drain(k, carry):
        @pl.when(is_mid)
        def _():
            own_raw(k).wait_send()
            onward_raw(k).wait_send()
            for i in range(2):
                own_to_end(k, i).wait_send()
                far_to_end(k, i).wait_send()
            mid_to_partner(k).wait_send()

        @pl.when(is_end)
        def _():
            end_raw(k).wait_send()
            end_to_partner(k).wait_send()

        return carry

    lax.fori_loop(0, steps, drain, 0)

    @pl.when(is_mid)
    def _():
        table_send(2, 0, chain.z_far_mid).wait_send()

    @pl.when(is_end)
    def _():
        table_send(1, 0, chain.z_mid).wait_send()
        table_send(3, 1, chain.z_far_mid).wait_send()


def forward_call(ids_t, weight_t, tokens, out_grad, w_gate, w_up, w_down, cap):
    count, depth = tokens.shape
    groups, ranks = lax.axis_size("dp"), lax.axis_size("expert")
    inner = w_gate.shape[2]
    width = depth // groups
    slot_rows = -(-cap // 16) * 16
    steps = 2 * groups
    hbm = pl.BlockSpec(memory_space=pl.ANY)
    vmem = pl.BlockSpec(memory_space=pltpu.VMEM)
    dma = pltpu.SemaphoreType.DMA
    blocked = jax.ShapeDtypeStruct((ranks, slot_rows, inner), BF16)
    return pl.pallas_call(
        functools.partial(forward_kernel, cap),
        out_shape=(
            jax.ShapeDtypeStruct((groups, width, inner), BF16),
            jax.ShapeDtypeStruct((groups, width, inner), BF16),
            jax.ShapeDtypeStruct((steps, ranks, slot_rows, width), BF16),
            blocked, blocked, blocked,
            jax.ShapeDtypeStruct((ranks, slot_rows, 128), F32),
            jax.ShapeDtypeStruct((4, 2 * ranks, count), F32),
        ),
        in_specs=[vmem, vmem, hbm, hbm, hbm, hbm, hbm],
        out_specs=(hbm, hbm, hbm, vmem, vmem, vmem, vmem, vmem),
        scratch_shapes=[
            pltpu.VMEM((4, steps, count, width), BF16),
            pltpu.VMEM((steps, ranks, slot_rows, width), BF16),
            pltpu.VMEM((steps, 4, slot_rows, width), BF16),
            pltpu.VMEM((steps, 2, 3, slot_rows, width), BF16),
            pltpu.VMEM((groups, width, inner), BF16),
            pltpu.VMEM((groups, width, inner), BF16),
            pltpu.VMEM((groups, inner, width), BF16),
            pltpu.VMEM((ranks, slot_rows, inner), F32),
            pltpu.VMEM((ranks, slot_rows, inner), F32),
            pltpu.VMEM((ranks, slot_rows, inner), F32),
            pltpu.VMEM((2, 4, 4 * slot_rows, count), BF16),
            dma((steps,)), dma((2, steps)), dma((3, steps)), dma((steps, 2, 2)), dma((steps, 2, 2)),
            dma((steps,)), dma((steps,)), dma((2,)), dma((3,)),
            dma((3,)), dma((3, 2)), dma((3, 2)), dma((3, 2)), dma((3, 2)), dma((3 + groups,)),
        ],
        compiler_params=pltpu.CompilerParams(
            collective_id=0, has_side_effects=True, vmem_limit_bytes=67000000
        ),
    )(ids_t, weight_t, tokens, out_grad, w_gate, w_up, w_down)


def swap(block, axis, distance):
    ranks = lax.axis_size(axis)
    return lax.ppermute(block, axis, [(rank, rank ^ distance) for rank in range(ranks)])


def any_mesh(tokens, out_grad, expert_ids, route_weight, w_gate, w_up, w_down):
    tok_count = tokens.shape[0]
    route_count = expert_ids.shape[1]
    ranks = lax.axis_size("expert")
    groups = lax.axis_size("dp")
    me = lax.axis_index("expert")
    group = lax.axis_index("dp")
    capacity = 3 * tok_count * route_count // (2 * ranks)
    routes = tok_count * route_count
    total_slots = ranks * capacity
    full_gate = lax.all_gather(w_gate[0], "dp", axis=0, tiled=True)
    full_up = lax.all_gather(w_up[0], "dp", axis=0, tiled=True)
    full_down = lax.all_gather(w_down[0], "dp", axis=1, tiled=True)
    half = ranks // 2
    flat_ids = expert_ids.reshape(routes)
    one_hot = (flat_ids[:, None] == jnp.arange(ranks, dtype=jnp.int32)[None, :]).astype(jnp.int32)
    slot_order = jnp.sum((jnp.cumsum(one_hot, axis=0) - 1) * one_hot, axis=1)
    slot_order = slot_order.reshape(tok_count, route_count)
    routing = jnp.concatenate(
        [
            expert_ids.astype(jnp.float32),
            slot_order.astype(jnp.float32),
            route_weight.astype(jnp.float32),
        ],
        axis=1,
    )
    far_routing = swap(routing, "expert", half)
    far_ids = far_routing[:, :route_count].astype(jnp.int32)
    far_order = far_routing[:, route_count : 2 * route_count].astype(jnp.int32)
    far_weight = far_routing[:, 2 * route_count :].astype(jnp.bfloat16)
    far_tokens = swap(tokens, "expert", half)
    late_grad, slot_order = lax.optimization_barrier((out_grad, slot_order))
    far_grad = swap(late_grad, "expert", half)
    slots = jnp.arange(total_slots, dtype=jnp.int32)

    def selectors(destination, weight, count):
        picks = jnp.zeros((count, tok_count), jnp.bfloat16)
        weighted = jnp.zeros((count, tok_count), jnp.bfloat16)
        for k in range(route_count):
            hit = slots[:count, None] == destination[:, k][None, :]
            picks = jnp.where(hit, jnp.ones((), jnp.bfloat16), picks)
            weighted = jnp.where(hit, weight[:, k][None, :], weighted)
        return picks, weighted

    destination = (expert_ids ^ me) * capacity + slot_order
    far_destination = (far_ids ^ me) * capacity + far_order
    near_slots = half * capacity
    picks, _ = selectors(destination, route_weight, total_slots)
    near_picks, near_weighted = selectors(destination, route_weight, near_slots)
    far_picks, far_weighted = selectors(far_destination, far_weight, near_slots)

    def blocks(buffer, count=ranks):
        return [buffer[d * capacity : (d + 1) * capacity] for d in range(count)]

    def exchange(buffer, count=ranks):
        return [
            swap(block, "expert", d) if d else block for d, block in enumerate(blocks(buffer, count))
        ]

    rows_in = jnp.concatenate(
        exchange(dot(near_picks, tokens, 1, 0).astype(jnp.bfloat16), half)
        + exchange(dot(far_picks, far_tokens, 1, 0).astype(jnp.bfloat16), half)
    )
    gate_value = dot(rows_in, full_gate, 1, 0)
    up_value = dot(rows_in, full_up, 1, 0)
    sigmoid_gate = jax.nn.sigmoid(gate_value)
    activated = gate_value * sigmoid_gate
    hidden = (activated * up_value).astype(jnp.bfloat16)
    scaled_blocks = exchange(
        dot(near_weighted, late_grad, 1, 0).astype(jnp.bfloat16), half
    ) + exchange(dot(far_weighted, far_grad, 1, 0).astype(jnp.bfloat16), half)
    scaled_blocks, hidden = lax.optimization_barrier((scaled_blocks, hidden))
    scaled = jnp.concatenate(scaled_blocks)
    hidden_grad = dot(scaled, full_down, 1, 1)
    gate_delta = (
        hidden_grad * up_value * sigmoid_gate * (1.0 + gate_value * (1.0 - sigmoid_gate))
    ).astype(jnp.bfloat16)
    up_delta = (hidden_grad * activated).astype(jnp.bfloat16)
    input_grad = (
        dot(gate_delta, full_gate, 1, 1) + dot(up_delta, full_up, 1, 1)
    ).astype(jnp.bfloat16)
    back_blocks = []
    for d, block in enumerate(blocks(input_grad)):
        back_blocks.append(swap(block, "expert", d) if d else block)
    down_part = dot(hidden, scaled, 0, 0).astype(jnp.bfloat16)
    input_grad, rows_in, hidden = lax.optimization_barrier((input_grad, rows_in, hidden))
    expert_out = dot(hidden, full_down, 1, 0)
    weighted_dot = jnp.sum(expert_out * scaled.astype(jnp.float32), axis=1)
    gate_part = dot(rows_in, gate_delta, 0, 0).astype(jnp.bfloat16)
    up_part = dot(rows_in, up_delta, 0, 0).astype(jnp.bfloat16)
    down_grad = lax.psum_scatter(down_part, "dp", scatter_dimension=1, tiled=True)[None]
    gate_grad = lax.psum_scatter(gate_part, "dp", scatter_dimension=0, tiled=True)[None]
    depth = up_part.shape[0] // groups
    up_sum = jnp.zeros((depth, up_part.shape[1]), jnp.float32)
    for d in range(groups):
        piece = lax.dynamic_slice_in_dim(up_part, (group ^ d) * depth, depth, 0)
        up_sum = up_sum + (swap(piece, "dp", d) if d else piece).astype(jnp.float32)
    up_grad = up_sum.astype(jnp.bfloat16)[None]

    token_sum = jnp.zeros(tokens.shape, jnp.float32)
    for pick, block in zip(blocks(picks), back_blocks):
        token_sum = token_sum + dot(pick, block, 0, 0)
    token_grad = token_sum.astype(jnp.bfloat16)

    order = jnp.arange(ranks, dtype=jnp.int32)
    dots = weighted_dot.reshape(ranks, capacity)
    by_rank = jnp.sum(
        jnp.where(((order ^ me)[:, None] == order[None, :])[:, :, None], dots[None], 0.0), axis=1
    )
    back_dots = lax.all_to_all(by_rank, "expert", split_axis=0, concat_axis=0, tiled=True)
    arrival = expert_ids * capacity + slot_order
    hits = arrival.reshape(tok_count, route_count, 1) == slots[None, None, :]
    own_dots = jnp.sum(jnp.where(hits, back_dots.reshape(total_slots)[None, None, :], 0.0), axis=2)
    route_grad = (own_dots / route_weight.astype(jnp.float32)).astype(jnp.bfloat16)
    return (token_grad, route_grad, gate_grad, up_grad, down_grad)


def on_device(tokens, out_grad, expert_ids, route_weight, w_gate, w_up, w_down):
    count, depth = tokens.shape
    top = expert_ids.shape[1]
    groups, ranks = lax.axis_size("dp"), lax.axis_size("expert")
    cap = 3 * count * top // (2 * ranks)
    fg, fu, rows, hidden, gd, ud, dots, table = forward_call(
        expert_ids.T, route_weight.T.astype(F32), tokens, out_grad, w_gate, w_up, w_down, cap)
    slot_rows = rows.shape[2]
    total = ranks * slot_rows
    inner = w_gate.shape[2]
    perm = [4 * (r % 2) + r // 2 for r in range(ranks)]
    perm = jnp.array(perm)
    x = rows[:groups].transpose(1, 2, 0, 3).reshape(ranks, slot_rows, depth)[perm].reshape(total, depth)
    sc = rows[groups:].transpose(1, 2, 0, 3).reshape(ranks, slot_rows, depth)[perm].reshape(total, depth)
    hidden, gd, ud = [v[perm].reshape(total, inner) for v in (hidden, gd, ud)]
    dots = dots[:, :, 0][perm]
    full_gate, full_up = fg.reshape(depth, inner), fu.reshape(depth, inner)
    gate_part = dot(x, gd, 0, 0).astype(BF16)
    up_part = dot(x, ud, 0, 0).astype(BF16)
    down_part = dot(hidden, sc, 0, 0).astype(BF16)
    down_grad = lax.psum_scatter(down_part, "dp", scatter_dimension=1, tiled=True)[None]
    gate_grad = lax.psum_scatter(gate_part, "dp", scatter_dimension=0, tiled=True)[None]
    up_grad = lax.psum_scatter(up_part, "dp", scatter_dimension=0, tiled=True)[None]
    ig = (dot(gd, full_gate, 1, 1) + dot(ud, full_up, 1, 1)).astype(BF16).reshape(ranks, slot_rows, depth)
    back = lax.all_to_all(ig, "expert", split_axis=0, concat_axis=0, tiled=True)
    back_dots = lax.all_to_all(dots, "expert", split_axis=0, concat_axis=0, tiled=True)
    slot = table[0, :ranks]
    pick = (slot[:, None, :] == jnp.arange(slot_rows, dtype=F32)[None, :, None])
    token_grad = dot(pick.astype(BF16).reshape(total, count), back.reshape(total, depth), 0, 0).astype(BF16)
    val = jnp.sum(jnp.where(pick, back_dots[:, :, None], 0.0), axis=1)
    hit = expert_ids.T[:, None, :] == jnp.arange(ranks)[None, :, None]
    rg = jnp.sum(jnp.where(hit, val[None], 0.0), axis=1).T
    route_grad = (rg / route_weight.astype(F32)).astype(BF16)
    return token_grad, route_grad, gate_grad, up_grad, down_grad


def solution(mesh):
    placed = (
        P(("dp", "expert"), None),
        P(("dp", "expert"), None),
        P(("dp", "expert"), None),
        P(("dp", "expert"), None),
        P("expert", "dp", None),
        P("expert", "dp", None),
        P("expert", None, "dp"),
    )
    chained = mesh.shape["expert"] == 8 and mesh.shape["dp"] == 4
    return jax.shard_map(
        on_device if chained else any_mesh, mesh=mesh, in_specs=placed,
        out_specs=(
            P(("dp", "expert"), None),
            P(("dp", "expert"), None),
            P("expert", "dp", None),
            P("expert", "dp", None),
            P("expert", None, "dp"),
        ),
        check_vma=False,
    )
```

profile of v0, /device:TPU:1, one launch (start us, length us, event | category | flops | bytes accessed | tf_op | source)
XLA Modules:
  0.0 340.8 jit_solution(10558025093830000296)
XLA Ops:
  7.2 0.0 reduce-scatter.8.cloned.1.call-start
  7.2 1.3 convert_bitcast_fusion.weight_ref
  8.5 0.7 pad_clamp_fusion
  9.1 150.6 %shard_map.119 = (bf16[4,512,768]{2,1,0:T(8,128)(2,1)}, bf16[4,512,768]{2,1,0:T(8,128)(2,1)}, bf16[8,8,128,512]{3,2,1,0:T(8,128)(2,1)}, bf16[8,128,768]{2,1,0:T(...) custom-call(s32[2,320]{1,0:T(2,128)} %bitcast.54, ...), custom_call_target="tpu_custom_call" | custom-call | tf_op jit(solution)/shard_map/pallas_call | solution.py:400
  159.7 5.9 %slice_bitcast_fusion = (bf16[8,128,4,512]{3,1,0,2:T(8,128)(2,1)}, bf16[8,128,4,512]{3,1,0,2:T(8,128)(2,1)}) fusion(bf16[8,8,128,512]{3,2,1,0:T(8,128)(2,1)} %get-tuple-element.19), kind=kLoop, calls=%fused_computation.10 | loop fusion | bytes 16777216 | tf_op jit(solution)/shard_map/transpose | solution.py:569
  165.6 6.6 %copy.34 = bf16[8,128,4,512]{1,3,2,0:T(8,128)(2,1)} copy(bf16[8,128,4,512]{3,1,0,2:T(8,128)(2,1)} %get-tuple-element.21) | data formatting | bytes 8388608 | tf_op jit(solution)/shard_map/transpose | solution.py:569
  172.2 0.6 gather_fusion.4
  172.9 5.2 %gather_fusion.5 = bf16[8,128,2048]{1,2,0:T(8,128)(2,1)} fusion(bf16[8,128,2048]{1,2,0:T(8,128)(2,1)} %bitcast.48, s32[1024]{0:T(1024)S(1)} %pad_clamp_fusion), kind=kCustom, calls=%fused_computation.5 | custom fusion | bytes 8388640 | tf_op jit(solution)/shard_map/gather | solution.py:569
  178.1 7.1 %bitcast_convert_fusion = bf16[768,2048]{1,0:T(8,128)(2,1)} fusion(bf16[8,128,768]{2,1,0:T(8,128)(2,1)S(1)} %gather_fusion.4, bf16[8,128,2048]{1,2,0:T(8,128)(2,1)} %gather_fusion.5), kind=kOutput, calls=%fused_computation.7 | convolution fusion | flops 3222798336 | bytes 8912896 | tf_op jit(solution)/shard_map/dot_general | solution.py:16
  185.2 0.0 reduce-scatter.8.cloned.1.call-update
  185.2 0.2 reduce-scatter.6.cloned.1.call-start
  185.4 1.2 copy-done.1
  186.6 0.6 gather_fusion.1
  187.2 6.5 %copy.30 = bf16[8,128,4,512]{1,3,2,0:T(8,128)(2,1)} copy(bf16[8,128,4,512]{3,1,0,2:T(8,128)(2,1)} %get-tuple-element.22) | data formatting | bytes 8388608 | tf_op jit(solution)/shard_map/transpose | solution.py:568
  193.7 6.5 %copy.31 = bf16[8,128,2048]{2,1,0:T(8,128)(2,1)} copy(bf16[8,128,2048]{1,2,0:T(8,128)(2,1)} %bitcast.49) | data formatting | bytes 8388608 | tf_op jit(solution)/shard_map/reshape | solution.py:568
  200.3 5.1 %gather_fusion.3 = bf16[8,128,2048]{2,1,0:T(8,128)(2,1)} fusion(bf16[8,128,2048]{2,1,0:T(8,128)(2,1)} %copy.31, s32[1024]{0:T(1024)S(1)} %pad_clamp_fusion), kind=kCustom, calls=%fused_computation.3 | custom fusion | bytes 8388640 | tf_op jit(solution)/shard_map/gather | solution.py:568
  205.4 7.5 %bitcast_convert_fusion.1 = bf16[2048,768]{1,0:T(8,128)(2,1)} fusion(bf16[8,128,2048]{2,1,0:T(8,128)(2,1)} %gather_fusion.3, bf16[8,128,768]{2,1,0:T(8,128)(2,1)S(1)} %gather_fusion.1), kind=kOutput, calls=%fused_computation.8 | convolution fusion | flops 3222798336 | bytes 8912896 | tf_op jit(solution)/shard_map/dot_general | solution.py:16
  212.9 0.0 reduce-scatter.6.cloned.1.call-update
  212.9 1.4 slice_reduce_fusion
  214.2 1.1 gather_fusion.2
  215.4 3.3 all-to-all-start.1
  218.7 1.8 gather_fusion
  220.5 6.0 %fusion.3 = f32[1024,2048]{1,0:T(8,128)S(1)} fusion(bf16[1024,768]{1,0:T(8,128)(2,1)} %bitcast.52, bf16[2048,768]{1,0:T(8,128)(2,1)} %bitcast.57), kind=kOutput, calls=%fused_computation.25 | convolution fusion | flops 3221225472 | bytes 13107200 | tf_op jit(solution)/shard_map/dot_general | solution.py:16
  226.5 5.1 %add_convert_fusion = bf16[1024,2048]{1,0:T(8,128)(2,1)} fusion(f32[1024,2048]{1,0:T(8,128)S(1)} %fusion.3, bf16[1024,768]{1,0:T(8,128)(2,1)S(1)} %bitcast.51, bf16[2048,768]{1,0:T(8,128)(2,1)S(1)} %bitcast.56), kind=kOutput, calls=%fused_computation.6 | convolution fusion | flops 3225419776 | bytes 17301504 | tf_op jit(solution)/shard_map/dot_general | solution.py:16
  231.6 4.7 %all-to-all-start = ((bf16[8,128,2048]{2,1,0:T(8,128)(2,1)}), bf16[8,128,2048]{2,1,0:T(8,128)(2,1)}, u32[]{:S(2)}, u32[]{:S(2)}) async-start(bf16[8,128,2048]{2,1,0:T(8,128)(2,1)} %bitcast.50), calls=%async_computation | async-start | bytes 8388608 | tf_op jit(solution)/shard_map/all_to_all | solution.py:580
  236.3 0.2 reduce-scatter.4.cloned.1.call-start
  236.5 7.9 %bitcast_convert_fusion.2 = bf16[2048,768]{1,0:T(8,128)(2,1)} fusion(bf16[8,128,2048]{2,1,0:T(8,128)(2,1)} %gather_fusion.3, bf16[8,128,768]{2,1,0:T(8,128)(2,1)S(1)} %copy-done.2), kind=kOutput, calls=%fused_computation.9 | convolution fusion | flops 3222798336 | bytes 8912896 | tf_op jit(solution)/shard_map/dot_general | solution.py:16
  244.4 0.7 slice_bitcast_fusion.2
  245.2 0.8 select_reduce_fusion
  246.0 0.6 fusion.2
  246.6 82.8 %all-to-all-done = bf16[8,128,2048]{2,1,0:T(8,128)(2,1)} async-done(((bf16[8,128,2048]{2,1,0:T(8,128)(2,1)}), bf16[8,128,2048]{2,1,0:T(8,128)(2,1)}, u32[]{:S(2)}, u32[]{:S(2)}) %all-to-all-start) | async-done | bytes 4194336 | tf_op jit(solution)/shard_map/all_to_all | solution.py:580
  329.4 4.8 %fusion = bf16[320,2048]{1,0:T(8,128)(2,1)} fusion(bf16[8,128,2048]{2,1,0:T(8,128)(2,1)} %all-to-all-done, f32[8,320]{1,0:T(8,128)S(1)} %slice_bitcast_fusion.2), kind=kOutput, calls=%fused_computation.13 | convolution fusion | flops 1343160320 | bytes 5515264 | tf_op jit(solution)/shard_map/dot_general | solution.py:16
  (19 shorter events, 0.1 us)
Async XLA Ops:
  7.2 327.1 %reduce-scatter.8.cloned.1.call-start = ((), (), s32[]{:S(2)}) async-start(), calls=%async_computation.7 | async-start | bytes 3932160 | tf_op jit(solution)/shard_map/reduce_scatter | solution.py:576
  165.6 6.6 %copy-start.3 = (bf16[8,128,768]{2,1,0:T(8,128)(2,1)S(1)}, bf16[8,128,768]{2,1,0:T(8,128)(2,1)}, u32[]{:S(2)}) copy-start(bf16[8,128,768]{2,1,0:T(8,128)(2,1)} %get-tuple-element.20) | copy-start | bytes 4718596
  185.2 1.4 copy-start.1
  185.2 149.1 %reduce-scatter.6.cloned.1.call-start = ((), (), s32[]{:S(2)}) async-start(), calls=%async_computation.6 | async-start | bytes 3932160 | tf_op jit(solution)/shard_map/reduce_scatter | solution.py:578
  212.8 5.8 %copy-start = (bf16[8,128,768]{2,1,0:T(8,128)(2,1)S(1)}, bf16[8,128,768]{2,1,0:T(8,128)(2,1)}, u32[]{:S(2)}) copy-start(bf16[8,128,768]{2,1,0:T(8,128)(2,1)} %get-tuple-element.14) | copy-start | bytes 4718596
  215.4 16.2 %all-to-all-start.1 = ((f32[8,1,128]{2,1,0:T(1,128)}), f32[8,1,128]{2,1,0:T(1,128)S(1)}, u32[]{:S(2)}, u32[]{:S(2)}) async-start(f32[8,1,128]{2,1,0:T(1,128)} %bitcast.10), calls=%async_computation.1 | async-start | bytes 8192 | tf_op jit(solution)/shard_map/all_to_all | solution.py:581
  220.5 6.0 %copy-start.6 = (bf16[4,512,768]{2,1,0:T(8,128)(2,1)S(1)}, bf16[4,512,768]{2,1,0:T(8,128)(2,1)}, u32[]{:S(2)}) copy-start(bf16[4,512,768]{2,1,0:T(8,128)(2,1)} %get-tuple-element.17) | copy-start | bytes 9437188
  231.6 4.9 %copy-start.2 = (bf16[8,128,768]{2,1,0:T(8,128)(2,1)S(1)}, bf16[8,128,768]{2,1,0:T(8,128)(2,1)}, u32[]{:S(2)}) copy-start(bf16[8,128,768]{2,1,0:T(8,128)(2,1)} %gather_fusion) | copy-start | bytes 4718596
  231.6 97.8 %all-to-all-start = ((bf16[8,128,2048]{2,1,0:T(8,128)(2,1)}), bf16[8,128,2048]{2,1,0:T(8,128)(2,1)}, u32[]{:S(2)}, u32[]{:S(2)}) async-start(bf16[8,128,2048]{2,1,0:T(8,128)(2,1)} %bitcast.50), calls=%async_computation | async-start | bytes 8388608 | tf_op jit(solution)/shard_map/all_to_all | solution.py:580
  236.3 97.9 %reduce-scatter.4.cloned.1.call-start = ((), (), s32[]{:S(2)}) async-start(), calls=%async_computation.5 | async-start | bytes 3932160 | tf_op jit(solution)/shard_map/reduce_scatter | solution.py:577
  244.4 1.6 copy-start.4
  244.4 1.6 copy-start.5
Sparse Core Ops, SparseCore 0:
  185.3 42.0 reduce-scatter.7
  231.0 43.8 reduce-scatter.5
  278.5 43.8 reduce-scatter.3
where the time goes:
time: 343 us; the launch traced here: 341 us
  Pallas kernels  151 us (44%)
  waiting for transfers between devices  82.9 us (24%)
  local copies, waits for them, and re-layouts  43.3 us (13%)
  matrix products  38.3 us (11%)
  between operations  13.8 us (4%)
  starting transfers between devices  8.44 us (2%)
    pallas_call x1, Pallas kernels, forward_call(): pl.pallas_call(functools.partial(forward_kernel, cap), out_shape=(jax.Sha...  151 us
    all_to_all x1, waiting for transfers between devices, on_device(): back = lax.all_to_all(ig, 'expert', split_axis=0, concat_axis=0, tiled=True)  82.8 us
    dot_general x6, matrix products, dot(): lax.dot_general(left, right, (((over_left,), (over_right,)), ((), ())), p...  38.3 us
    transpose x2, local copies, waits for them, and re-layouts, on_device(): rows[groups:].transpose(1, 2, 0, 3).reshape(ranks, slot_rows, depth)[perm]  12.5 us
  transfers between devices with their start and end apart: 5, of which 1 were waited for; matrix products, arithmetic and copies ran while one was open for 17% of the time, Pallas kernels for 0%

commit v1 on v0

--- a/solution.py
+++ b/solution.py
@@ -67,7 +67,7 @@
 def forward_kernel(
     cap,
     ids_ref, weight_ref, tokens_ref, grads_ref, wg_ref, wu_ref, wd_ref,
-    full_gate_out, full_up_out, rows_out, hidden_out, gate_delta_out, up_delta_out, dots_out, table_out,
+    full_out, rows_out, hidden_out, delta_out, dots_out, table_out,
     raw, rows, stage_d, stage_e, full_gate, full_up, full_down, gate_val, up_val, hg_val, select,
     load_sem, raw_ss, raw_rs, e_ss, e_rs, d_ss, d_rs, tab_ss, tab_rs,
     w_ls, wa_ss, wa_rs, wf_ss, wf_rs, out_sem,
@@ -287,23 +287,22 @@
 
         @pl.when(k >= groups + 1)
         def _():
-            b = 2 * (k - groups - 1)
-            for half in range(2):
-                block = b + half
-                piece = [rows[kk, block] for kk in range(groups)]
-                gate = functools.reduce(jnp.add, [dot(piece[kk], full_gate[kk]) for kk in range(groups)])
-                up = functools.reduce(jnp.add, [dot(piece[kk], full_up[kk]) for kk in range(groups)])
-                gate_val[block] = gate
-                up_val[block] = up
-                hidden_out[block] = (gate * jax.nn.sigmoid(gate) * up).astype(BF16)
+            pair = pl.ds(2 * (k - groups - 1), 2)
+            shape = (2, slot_rows, gate_val.shape[2])
+            piece = [rows[kk, pair].reshape(2 * slot_rows, width) for kk in range(groups)]
+            gate = functools.reduce(jnp.add, [dot(piece[kk], full_gate[kk]) for kk in range(groups)])
+            up = functools.reduce(jnp.add, [dot(piece[kk], full_up[kk]) for kk in range(groups)])
+            gate_val[pair] = gate.reshape(shape)
+            up_val[pair] = up.reshape(shape)
+            hidden_out[pair] = (gate * jax.nn.sigmoid(gate) * up).astype(BF16).reshape(shape)
 
         return carry
 
     lax.fori_loop(0, steps + 1, step, 0)
 
     outs = [
-        pltpu.make_async_copy(full_gate, full_gate_out, out_sem.at[0]),
-        pltpu.make_async_copy(full_up, full_up_out, out_sem.at[1]),
+        pltpu.make_async_copy(full_gate, full_out.at[0], out_sem.at[0]),
+        pltpu.make_async_copy(full_up, full_out.at[1], out_sem.at[1]),
     ]
     for copy in outs:
         copy.start()
@@ -319,30 +318,31 @@
         pltpu.make_async_copy(rows.at[groups + q], rows_out.at[groups + q], out_sem.at[3 + q]).start()
 
         def tile(t, carry):
-            value = dot(rows[groups + q, t], full_down[q], 1, 1)
+            four = pl.ds(4 * t, 4)
+            left = rows[groups + q, four].reshape(4 * slot_rows, width)
+            value = dot(left, full_down[q], 1, 1).reshape(4, slot_rows, hg_val.shape[2])
 
             @pl.when(q == 0)
             def _():
-                hg_val[t] = value
+                hg_val[four] = value
 
             @pl.when(q > 0)
             def _():
-                hg_val[t] += value
+                hg_val[four] += value
 
             return carry
 
-        return lax.fori_loop(0, ranks, tile, carry)
+        return lax.fori_loop(0, ranks // 4, tile, carry)
 
     lax.fori_loop(0, groups, hidden_grad, 0)
 
     def deltas(t, carry):
         gate, up, grad = gate_val[t], up_val[t], hg_val[t]
         sig = jax.nn.sigmoid(gate)
-        gate_delta_out[t] = (grad * up * sig * (1.0 + gate * (1.0 - sig))).astype(BF16)
-        up_delta_out[t] = (grad * (gate * sig)).astype(BF16)
-        dots_out[t] = jnp.broadcast_to(
-            jnp.sum(hidden_out[t].astype(F32) * grad, axis=1, keepdims=True), dots_out.shape[1:]
-        )
+        delta_out[0, t] = (grad * up * sig * (1.0 + gate * (1.0 - sig))).astype(BF16)
+        delta_out[1, t] = (grad * (gate * sig)).astype(BF16)
+        total = jnp.sum(hidden_out[t].astype(F32) * grad, axis=1, keepdims=True)
+        dots_out[t] = jnp.broadcast_to(total, (total.shape[0], total.shape[0])).T[0:8, :]
         return carry
 
     lax.fori_loop(0, ranks, deltas, 0)
@@ -396,19 +396,18 @@
     hbm = pl.BlockSpec(memory_space=pl.ANY)
     vmem = pl.BlockSpec(memory_space=pltpu.VMEM)
     dma = pltpu.SemaphoreType.DMA
-    blocked = jax.ShapeDtypeStruct((ranks, slot_rows, inner), BF16)
     return pl.pallas_call(
         functools.partial(forward_kernel, cap),
         out_shape=(
-            jax.ShapeDtypeStruct((groups, width, inner), BF16),
-            jax.ShapeDtypeStruct((groups, width, inner), BF16),
+            jax.ShapeDtypeStruct((2, groups, width, inner), BF16),
             jax.ShapeDtypeStruct((steps, ranks, slot_rows, width), BF16),
-            blocked, blocked, blocked,
-            jax.ShapeDtypeStruct((ranks, slot_rows, 128), F32),
+            jax.ShapeDtypeStruct((ranks, slot_rows, inner), BF16),
+            jax.ShapeDtypeStruct((2, ranks, slot_rows, inner), BF16),
+            jax.ShapeDtypeStruct((ranks, 8, slot_rows), F32),
             jax.ShapeDtypeStruct((4, 2 * ranks, count), F32),
         ),
         in_specs=[vmem, vmem, hbm, hbm, hbm, hbm, hbm],
-        out_specs=(hbm, hbm, hbm, vmem, vmem, vmem, vmem, vmem),
+        out_specs=(hbm, hbm, vmem, vmem, vmem, vmem),
         scratch_shapes=[
             pltpu.VMEM((4, steps, count, width), BF16),
             pltpu.VMEM((steps, ranks, slot_rows, width), BF16),
@@ -429,6 +428,392 @@
             collective_id=0, has_side_effects=True, vmem_limit_bytes=67000000
         ),
     )(ids_t, weight_t, tokens, out_grad, w_gate, w_up, w_down)
+
+
+def backward_kernel(
+    cap,
+    ids_ref, weight_ref, table_ref, dots_ref, full_ref, rows_ref, hidden_ref, delta_ref,
+    token_out, route_out, gate_out, up_out, down_out,
+    full, rows, hidden, delta, grads, comb, gf_send, gf_in, end_send, select,
+    diag_gu, diag_d, pair_gu, pair_d, relay_gu, relay_d, in_gu, in_d, dots_in,
+    load_sem, d_ss, d_rs, far_ss, far_rs, near_ss, near_rs, gf_ss, gf_rs, es_ss, es_rs,
+    dots_ss, dots_rs, relay_ss, relay_rs, pair_ss, pair_rs,
+):
+    chain = Chain()
+    g, me, c, z = chain.g, chain.me, chain.c, chain.z
+    is_mid, is_end = chain.is_mid, chain.is_end
+    groups = lax.axis_size("dp")
+    ranks = lax.axis_size("expert")
+    _, slot_rows, width = rows.shape[1:]
+    count = table_ref.shape[2]
+    inner = hidden.shape[2]
+    along_x, along_y = neighbours(g)
+    across = groups - 1 - g
+    slots = ranks * slot_rows
+
+    loads = [
+        pltpu.make_async_copy(delta_ref, delta, load_sem.at[0]),
+        pltpu.make_async_copy(rows_ref.at[across], rows.at[across], load_sem.at[1]),
+        pltpu.make_async_copy(full_ref.at[:, 0], full.at[:, 0], load_sem.at[2]),
+        pltpu.make_async_copy(hidden_ref, hidden, load_sem.at[3]),
+        pltpu.make_async_copy(rows_ref.at[groups + across], rows.at[groups + across], load_sem.at[4]),
+        pltpu.make_async_copy(full_ref.at[:, pl.ds(1, groups - 1)], full.at[:, pl.ds(1, groups - 1)], load_sem.at[5]),
+    ]
+    for i, shard in enumerate((along_x, along_y, g)):
+        loads.append(pltpu.make_async_copy(rows_ref.at[shard], rows.at[shard], load_sem.at[6 + i]))
+        loads.append(
+            pltpu.make_async_copy(rows_ref.at[groups + shard], rows.at[groups + shard], load_sem.at[9 + i])
+        )
+    for copy in loads:
+        copy.start()
+
+    greet(chain, ranks, groups)
+
+    real = pl.ds(0, cap)
+
+    def dots_to(peer):
+        return send(
+            dots_ref.at[4 * (peer % 2) + peer // 2], dots_in.at[me],
+            dots_ss.at[peer], dots_rs.at[me], (g, peer),
+        )
+
+    def dots_from(peer):
+        return send(
+            dots_ref.at[4 * c + z], dots_in.at[peer], dots_ss.at[peer], dots_rs.at[peer], (g, peer)
+        )
+
+    for step in range(1, ranks):
+        dots_to((me + step) % ranks).start()
+
+    comb[:, :, :, cap:, :] = jnp.zeros((groups, 4, 4, slot_rows - cap, width), BF16)
+    targets = (me, me + 1 - 2 * c, 2 * chain.z_near, 2 * chain.z_near + 1)
+
+    def selectors(j, z_from):
+        slot = lax.broadcasted_iota(jnp.int32, (slot_rows, count), 0).astype(F32)
+        for i, rank in enumerate(targets):
+            hit = table_ref[j, pl.ds(rank, 1), :] == slot
+            select[z_from, i * slot_rows : (i + 1) * slot_rows, :] = jnp.where(hit, 1.0, 0.0).astype(BF16)
+
+    selectors(0, z)
+
+    @pl.when(is_mid)
+    def _():
+        selectors(1, chain.z_end)
+        selectors(2, chain.z_far_mid)
+        selectors(3, chain.z_far_end)
+
+    def to_partner(k):
+        return send(
+            grads.at[k, pl.ds(4 * (1 - c), 4), real], comb.at[k, :, 1, real],
+            d_ss.at[k], d_rs.at[k], chain.at(z, 1 - c),
+        )
+
+    def end_to_partner(k):
+        return send(
+            grads.at[k, 4 * (1 - c) + z, real], comb.at[k, z, 1, real],
+            d_ss.at[k], d_rs.at[k], chain.at(z, 1 - c),
+        )
+
+    def far_home(k, core):
+        return send(
+            grads.at[k, pl.ds(4 * core + 2 * chain.far, 2), real],
+            comb.at[k, pl.ds(2 * chain.far, 2), 2 + c, real],
+            far_ss.at[k, core], far_rs.at[k, c], chain.at(chain.z_mid, core),
+        )
+
+    def far_from(k, core):
+        return send(
+            grads.at[k, pl.ds(4 * core + 2 * chain.far, 2), real],
+            comb.at[k, pl.ds(2 * chain.far, 2), 2 + core, real],
+            far_ss.at[k, core], far_rs.at[k, core], chain.at(chain.z_end, core),
+        )
+
+    def near_home(k, core):
+        return send(
+            grads.at[k, 4 * core + chain.z_mid, real], comb.at[k, chain.z_mid, 2 + c, real],
+            near_ss.at[k, core], near_rs.at[k, c], chain.at(chain.z_mid, core),
+        )
+
+    def near_from(k, core):
+        return send(
+            grads.at[k, 4 * core + chain.z_mid, real], comb.at[k, chain.z_mid, 2 + core, real],
+            near_ss.at[k, core], near_rs.at[k, core], chain.at(chain.z_end, core),
+        )
+
+    def sums_across(k):
+        return send(gf_send.at[k], gf_in.at[k], gf_ss.at[k], gf_rs.at[k], chain.at(chain.z_far_mid, c))
+
+    def sums_to_end(k):
+        return send(end_send.at[k], gf_in.at[k, 0], es_ss.at[k], es_rs.at[k], chain.at(chain.z_end, c))
+
+    def device_on(way):
+        return ((along_x if way == 0 else along_y), me)
+
+    def relay_to(w, way):
+        if w == 2:
+            half = diag_d.shape[0] // 2
+            src, dst = diag_d.at[pl.ds(way * half, half)], relay_d.at[way]
+        else:
+            half = diag_gu.shape[1] // 2
+            src, dst = diag_gu.at[w, pl.ds(way * half, half)], relay_gu.at[w, way]
+        return send(src, dst, relay_ss.at[w, way], relay_rs.at[w, way], device_on(way))
+
+    def pair_to(w, way):
+        src, dst = (pair_d.at[way], in_d.at[way]) if w == 2 else (pair_gu.at[w, way], in_gu.at[w, way])
+        return send(src, dst, pair_ss.at[w, way], pair_rs.at[w, way], device_on(way))
+
+    def part(w, shard, tile):
+        if w == 2:
+            half = inner // 2
+            left = hidden[:, :, pl.ds(tile * half, half)].reshape(slots, half)
+            return dot(left, rows[groups + shard].reshape(slots, width), 0, 0)
+        half = width // 2
+        left = rows[shard, :, :, pl.ds(tile * half, half)].reshape(slots, half)
+        return dot(left, delta[w].reshape(slots, inner), 0, 0)
+
+    def over_two(body):
+        for tile in range(2):
+            body(tile)
+
+    def diagonal(w):
+        def body(tile):
+            value = part(w, across, tile).astype(BF16)
+            half = value.shape[0]
+            if w == 2:
+                diag_d[pl.ds(tile * half, half), :] = value
+            else:
+                diag_gu[w, pl.ds(tile * half, half), :] = value
+
+        over_two(body)
+        for way in range(2):
+            relay_to(w, way).start()
+
+    def pairs(w):
+        for way in range(2):
+            shard = along_x if way == 0 else along_y
+            relay_to(w, 1 - way).wait_recv()
+
+            def body(tile):
+                value = part(w, shard, tile)
+                half = value.shape[0]
+                if tile == 1 - way:
+                    come = relay_d[1 - way] if w == 2 else relay_gu[w, 1 - way]
+                    value = value.astype(BF16).astype(F32) + come.astype(F32)
+                value = value.astype(BF16)
+                if w == 2:
+                    pair_d[way, pl.ds(tile * half, half), :] = value
+                else:
+                    pair_gu[w, way, pl.ds(tile * half, half), :] = value
+
+            over_two(body)
+            pair_to(w, way).start()
+
+    def finish(w):
+        for way in range(2):
+            pair_to(w, way).wait_recv()
+
+        def body(tile):
+            value = part(w, g, tile)
+            half = value.shape[0]
+            block = pl.ds(tile * half, half)
+            for way in range(2):
+                come = in_d[way, block, :] if w == 2 else in_gu[w, way, block, :]
+                value = value + come.astype(F32)
+            (gate_out, up_out, down_out)[w][block, :] = value.astype(BF16)
+
+        over_two(body)
+
+    def input_grad(k):
+        for hc in range(2):
+            left = [delta[w, pl.ds(4 * hc, 4)].reshape(4 * slot_rows, inner) for w in range(2)]
+            value = (dot(left[0], full[0, k], 1, 1) + dot(left[1], full[1, k], 1, 1)).astype(BF16)
+            value = value.reshape(4, slot_rows, width)
+            grads[k, pl.ds(4 * hc, 4)] = value
+
+            @pl.when(c == hc)
+            def _():
+                comb[k, :, 0] = value
+
+    def summed(k, z_from, blocks):
+        return dot(
+            select[z_from, 0 : blocks * slot_rows, :],
+            comb[k, z_from, 0:blocks].reshape(blocks * slot_rows, width), 0, 0,
+        )
+
+    for i in range(3):
+        loads[i].wait()
+
+    def first(k, carry):
+        for w in range(3):
+            @pl.when(k == w)
+            def _():
+                if w == 2:
+                    loads[3].wait()
+                    loads[4].wait()
+                diagonal(w)
+
+        @pl.when(k == 1)
+        def _():
+            loads[5].wait()
+
+        input_grad(k)
+
+        @pl.when(is_mid)
+        def _():
+            to_partner(k).start()
+
+        @pl.when(is_end)
+        def _():
+            for core in range(2):
+                far_home(k, core).start()
+            end_to_partner(k).start()
+
+        return carry
+
+    lax.fori_loop(0, groups, first, 0)
+
+    @pl.when(is_end)
+    def _():
+        for k in range(groups):
+            for core in range(2):
+                near_home(k, core).start()
+
+    for copy in loads[6:]:
+        copy.wait()
+
+    def second(k, carry):
+        for w in range(3):
+            @pl.when(k == w)
+            def _():
+                pairs(w)
+
+        @pl.when(is_mid)
+        def _():
+            to_partner(k).wait_recv()
+            for core in range(2):
+                far_from(k, core).wait_recv()
+            gf_send[k, 0] = summed(k, chain.z_far_mid, 4).astype(BF16)
+            gf_send[k, 1] = summed(k, chain.z_far_end, 4).astype(BF16)
+            sums_across(k).start()
+
+        return carry
+
+    lax.fori_loop(0, groups, second, 0)
+
+    for step in range(1, ranks):
+        dots_from((me + step) % ranks).wait_recv()
+    dots_in[me] = dots_ref[4 * c + z]
+    found = jnp.zeros(route_out.shape, F32)
+    slot = lax.broadcasted_iota(jnp.int32, (slot_rows, count), 0).astype(F32)
+    for rank in range(ranks):
+        hit = jnp.where(table_ref[0, rank : rank + 1, :] == slot, 1.0, 0.0)
+        value = lax.dot_general(
+            dots_in[rank], hit, (((1,), (0,)), ((), ())),
+            precision=lax.Precision.HIGHEST, preferred_element_type=F32,
+        )[0:1, :]
+        found = jnp.where(ids_ref[...] == rank, value, found)
+    route_out[...] = found / weight_ref[...]
+
+    def third(k, carry):
+        columns = pl.ds(pl.multiple_of(k * width, 128), width)
+
+        @pl.when(is_mid)
+        def _():
+            sums_across(k).wait_recv()
+            end_send[k] = (summed(k, chain.z_end, 2) + gf_in[k, 1].astype(F32)).astype(BF16)
+            sums_to_end(k).start()
+            for core in range(2):
+                near_from(k, core).wait_recv()
+            token_out[:, columns] = (summed(k, z, 4) + gf_in[k, 0].astype(F32)).astype(BF16)
+
+        for w in range(3):
+            @pl.when(k == w + 1)
+            def _():
+                finish(w)
+
+        @pl.when(is_end)
+        def _():
+            end_to_partner(k).wait_recv()
+            sums_to_end(k).wait_recv()
+            token_out[:, columns] = (summed(k, z, 2) + gf_in[k, 0].astype(F32)).astype(BF16)
+
+        return carry
+
+    lax.fori_loop(0, groups, third, 0)
+
+    for w in range(3):
+        for way in range(2):
+            relay_to(w, way).wait_send()
+            pair_to(w, way).wait_send()
+    for step in range(1, ranks):
+        dots_to((me + step) % ranks).wait_send()
+
+    def drain(k, carry):
+        @pl.when(is_mid)
+        def _():
+            to_partner(k).wait_send()
+            sums_across(k).wait_send()
+            sums_to_end(k).wait_send()
+
+        @pl.when(is_end)
+        def _():
+            for core in range(2):
+                far_home(k, core).wait_send()
+                near_home(k, core).wait_send()
+            end_to_partner(k).wait_send()
+
+        return carry
+
+    lax.fori_loop(0, groups, drain, 0)
+
+
+def backward_call(ids_t, weight_t, table, dots, full, rows, hidden, delta, cap):
+    groups, ranks = lax.axis_size("dp"), lax.axis_size("expert")
+    _, _, slot_rows, width = rows.shape
+    count = table.shape[2]
+    inner = hidden.shape[2]
+    hbm = pl.BlockSpec(memory_space=pl.ANY)
+    vmem = pl.BlockSpec(memory_space=pltpu.VMEM)
+    dma = pltpu.SemaphoreType.DMA
+    return pl.pallas_call(
+        functools.partial(backward_kernel, cap),
+        out_shape=(
+            jax.ShapeDtypeStruct((count, groups * width), BF16),
+            jax.ShapeDtypeStruct(ids_t.shape, F32),
+            jax.ShapeDtypeStruct((width, inner), BF16),
+            jax.ShapeDtypeStruct((width, inner), BF16),
+            jax.ShapeDtypeStruct((inner, width), BF16),
+        ),
+        in_specs=[vmem, vmem, vmem, vmem, hbm, hbm, hbm, hbm],
+        out_specs=(vmem,) * 5,
+        scratch_shapes=[
+            pltpu.VMEM(full.shape, BF16),
+            pltpu.VMEM(rows.shape, BF16),
+            pltpu.VMEM(hidden.shape, BF16),
+            pltpu.VMEM(delta.shape, BF16),
+            pltpu.VMEM((groups, ranks, slot_rows, width), BF16),
+            pltpu.VMEM((groups, 4, 4, slot_rows, width), BF16),
+            pltpu.VMEM((groups, 2, count, width), BF16),
+            pltpu.VMEM((groups, 2, count, width), BF16),
+            pltpu.VMEM((groups, count, width), BF16),
+            pltpu.VMEM((4, 4 * slot_rows, count), BF16),
+            pltpu.VMEM((2, width, inner), BF16),
+            pltpu.VMEM((inner, width), BF16),
+            pltpu.VMEM((2, 2, width, inner), BF16),
+            pltpu.VMEM((2, inner, width), BF16),
+            pltpu.VMEM((2, 2, width // 2, inner), BF16),
+            pltpu.VMEM((2, inner // 2, width), BF16),
+            pltpu.VMEM((2, 2, width, inner), BF16),
+            pltpu.VMEM((2, inner, width), BF16),
+            pltpu.VMEM(dots.shape, F32),
+            dma((12,)), dma((groups,)), dma((groups,)), dma((groups, 2)), dma((groups, 2)),
+            dma((groups, 2)), dma((groups, 2)), dma((groups,)), dma((groups,)), dma((groups,)), dma((groups,)),
+            dma((ranks,)), dma((ranks,)), dma((3, 2)), dma((3, 2)), dma((3, 2)), dma((3, 2)),
+        ],
+        compiler_params=pltpu.CompilerParams(
+            collective_id=1, has_side_effects=True, vmem_limit_bytes=67000000
+        ),
+    )(ids_t, weight_t, table, dots, full, rows, hidden, delta)
 
 
 def swap(block, axis, distance):
@@ -554,39 +939,16 @@
 
 
 def on_device(tokens, out_grad, expert_ids, route_weight, w_gate, w_up, w_down):
-    count, depth = tokens.shape
-    top = expert_ids.shape[1]
-    groups, ranks = lax.axis_size("dp"), lax.axis_size("expert")
-    cap = 3 * count * top // (2 * ranks)
-    fg, fu, rows, hidden, gd, ud, dots, table = forward_call(
-        expert_ids.T, route_weight.T.astype(F32), tokens, out_grad, w_gate, w_up, w_down, cap)
-    slot_rows = rows.shape[2]
-    total = ranks * slot_rows
-    inner = w_gate.shape[2]
-    perm = [4 * (r % 2) + r // 2 for r in range(ranks)]
-    perm = jnp.array(perm)
-    x = rows[:groups].transpose(1, 2, 0, 3).reshape(ranks, slot_rows, depth)[perm].reshape(total, depth)
-    sc = rows[groups:].transpose(1, 2, 0, 3).reshape(ranks, slot_rows, depth)[perm].reshape(total, depth)
-    hidden, gd, ud = [v[perm].reshape(total, inner) for v in (hidden, gd, ud)]
-    dots = dots[:, :, 0][perm]
-    full_gate, full_up = fg.reshape(depth, inner), fu.reshape(depth, inner)
-    gate_part = dot(x, gd, 0, 0).astype(BF16)
-    up_part = dot(x, ud, 0, 0).astype(BF16)
-    down_part = dot(hidden, sc, 0, 0).astype(BF16)
-    down_grad = lax.psum_scatter(down_part, "dp", scatter_dimension=1, tiled=True)[None]
-    gate_grad = lax.psum_scatter(gate_part, "dp", scatter_dimension=0, tiled=True)[None]
-    up_grad = lax.psum_scatter(up_part, "dp", scatter_dimension=0, tiled=True)[None]
-    ig = (dot(gd, full_gate, 1, 1) + dot(ud, full_up, 1, 1)).astype(BF16).reshape(ranks, slot_rows, depth)
-    back = lax.all_to_all(ig, "expert", split_axis=0, concat_axis=0, tiled=True)
-    back_dots = lax.all_to_all(dots, "expert", split_axis=0, concat_axis=0, tiled=True)
-    slot = table[0, :ranks]
-    pick = (slot[:, None, :] == jnp.arange(slot_rows, dtype=F32)[None, :, None])
-    token_grad = dot(pick.astype(BF16).reshape(total, count), back.reshape(total, depth), 0, 0).astype(BF16)
-    val = jnp.sum(jnp.where(pick, back_dots[:, :, None], 0.0), axis=1)
-    hit = expert_ids.T[:, None, :] == jnp.arange(ranks)[None, :, None]
-    rg = jnp.sum(jnp.where(hit, val[None], 0.0), axis=1).T
-    route_grad = (rg / route_weight.astype(F32)).astype(BF16)
-    return token_grad, route_grad, gate_grad, up_grad, down_grad
+    count = tokens.shape[0]
+    cap = 3 * count * expert_ids.shape[1] // (2 * lax.axis_size("expert"))
+    ids_t, weight_t = expert_ids.T, route_weight.T.astype(F32)
+    full, rows, hidden, delta, dots, table = forward_call(
+        ids_t, weight_t, tokens, out_grad, w_gate, w_up, w_down, cap
+    )
+    token_grad, route_grad, gate_grad, up_grad, down_grad = backward_call(
+        ids_t, weight_t, table, dots, full, rows, hidden, delta, cap
+    )
+    return token_grad, route_grad.T.astype(BF16), gate_grad[None], up_grad[None], down_grad[None]
 
 
 def solution(mesh):

time: 343 us -> 245 us (0.71)
  Pallas kernels: 151 us -> 236 us
  waiting for transfers between devices: 82.9 us -> 0 us
  matrix products: 38.3 us -> 0 us
  local copies, waits for them, and re-layouts: 43.3 us -> 5.24 us
  between operations: 13.8 us -> 0.66 us
  starting transfers between devices: 8.44 us -> 0 us
    pallas_call x0 -> x1, Pallas kernels: none -> 87.6 us  [backward_call(): pl.pallas_call(functools.partial(backward_kernel, cap), out_shape=(jax.Sh...]
    all_to_all x2 -> x0, waiting for transfers between devices: 82.8 us -> none  [the longest x1 82.8 us: on_device(): back = lax.all_to_all(ig, 'expert', split_axis=0, concat_axis=0, tiled=True)]
    dot_general x6 -> x0, matrix products: 38.3 us -> none  [dot(): lax.dot_general(left, right, (((over_left,), (over_right,)), ((), ())), p...]
    transpose x3 -> x0, local copies, waits for them, and re-layouts: 18.9 us -> none  [the longest x2 12.5 us: on_device(): rows[groups:].transpose(1, 2, 0, 3).reshape(ranks, slot_rows, depth)[perm]]
    gather x6 -> x0, local copies, waits for them, and re-layouts: 14.6 us -> none  [the longest x1 5.24 us: on_device(): rows[groups:].transpose(1, 2, 0, 3).reshape(ranks, slot_rows, depth)[perm]]
    all_to_all x2 -> x0, starting transfers between devices: 7.99 us -> none  [the longest x1 4.73 us: on_device(): back = lax.all_to_all(ig, 'expert', split_axis=0, concat_axis=0, tiled=True)]
    reshape x1 -> x0, local copies, waits for them, and re-layouts: 6.54 us -> none  [on_device(): rows[:groups].transpose(1, 2, 0, 3).reshape(ranks, slot_rows, depth)[perm]]
    unnamed x14 -> x10, local copies, waits for them, and re-layouts: 1.18 us -> 5.24 us
  transfers between devices with their start and end apart: 5 -> 0, of which waited for: 1 -> 0; matrix products, arithmetic and copies ran while one was open for 17% -> 0% of each run, Pallas kernels for 0% -> 0%
where the time goes in v1:
time: 245 us
  Pallas kernels  236 us (96%)
  local copies, waits for them, and re-layouts  5.24 us (2%)
  other arithmetic  2.57 us (1%)
    pallas_call x1, Pallas kernels, forward_call(): pl.pallas_call(functools.partial(forward_kernel, cap), out_shape=(jax.Sha...  149 us
    pallas_call x1, Pallas kernels, backward_call(): pl.pallas_call(functools.partial(backward_kernel, cap), out_shape=(jax.Sh...  87.6 us
    unnamed x10, local copies, waits for them, and re-layouts  5.24 us

profile of v1, /device:TPU:1, one launch (start us, length us, event | category | flops | bytes accessed | tf_op | source)
XLA Modules:
  0.0 245.0 jit_solution(14380404083855011861)
XLA Ops:
  0.6 1.3 convert_bitcast_fusion.weight_ref
  1.9 148.8 %shard_map.110 = (bf16[2,4,512,768]{3,2,1,0:T(8,128)(2,1)}, bf16[8,8,128,512]{3,2,1,0:T(8,128)(2,1)}, bf16[8,128,768]{2,1,0:T(8,128)(2,1)}, bf16[2,8,128,768]{3,...) custom-call(s32[2,320]{1,0:T(2,128)} %bitcast.11, f32[2,320]{1,0:T(2,128)} %convert_bitcast_fusion.weight_ref, ...), custom_call_target="tpu_custom_call" | custom-call | tf_op jit(solution)/shard_map/pallas_call | solution.py:399
  150.7 87.6 %shard_map.111 = (bf16[320,2048]{1,0:T(8,128)(2,1)}, f32[2,320]{1,0:T(2,128)}, bf16[512,768]{1,0:T(8,128)(2,1)}, bf16[512,768]{1,0:T(8,128)(2,1)}, bf16[768,512]{1,0:T(8,128)(2,1)}) custom-call(s32[2,320]{1,0:T(2,128)} %bitcast.12, f32[2,320]{1,0:T(2,128)} %convert_bitcast_fusion.weight_ref, f32[4,16,320]{2,1,0:T(8,128)} %get-tuple-element.16.table_ref, ...), custom_call_target="tpu_custom_call" | custom-call | tf_op jit(solution)/shard_map/pallas_call | solution.py:778
  238.4 0.0 copy-start.2
  238.4 1.3 convert_bitcast_fusion.1
  239.7 0.0 copy-start.1
  239.7 2.6 %copy.16 = bf16[320,2048]{1,0:T(8,128)(2,1)} copy(bf16[320,2048]{1,0:T(8,128)(2,1)} %get-tuple-element.32) | data formatting | bytes 2621440
  242.3 0.0 copy-done.2
  242.3 0.0 copy-start
  242.3 0.9 copy.17
  243.2 0.0 copy-done.1
  243.2 0.9 copy.18
  244.1 0.0 copy-done
  244.1 0.9 copy.19
Async XLA Ops:
  238.4 3.9 %copy-start.2 = (bf16[512,768]{1,0:T(8,128)(2,1)S(1)}, bf16[512,768]{1,0:T(8,128)(2,1)}, u32[]{:S(2)}) copy-start(bf16[512,768]{1,0:T(8,128)(2,1)} %get-tuple-element.24) | copy-start | bytes 2359300
  239.7 3.5 %copy-start.1 = (bf16[512,768]{1,0:T(8,128)(2,1)S(1)}, bf16[512,768]{1,0:T(8,128)(2,1)}, u32[]{:S(2)}) copy-start(bf16[512,768]{1,0:T(8,128)(2,1)} %get-tuple-element.25) | copy-start | bytes 2359300
  242.3 1.8 copy-start

commit v2 on v1

--- a/solution.py
+++ b/solution.py
@@ -38,7 +38,7 @@
         return (self.g, 2 * z + c)
 
 
-def greet(chain, ranks, groups):
+def greet(chain, ranks, groups, meanwhile=None):
     barrier = pltpu.get_barrier_semaphore()
     for step in range(1, ranks):
         pl.semaphore_signal(
@@ -48,6 +48,8 @@
         pl.semaphore_signal(
             barrier, inc=1, device_id=((chain.g + step) % groups, chain.me), device_id_type=MESH
         )
+    if meanwhile is not None:
+        meanwhile()
     pl.semaphore_wait(barrier, ranks + groups - 2)
 
 
@@ -67,10 +69,11 @@
 def forward_kernel(
     cap,
     ids_ref, weight_ref, tokens_ref, grads_ref, wg_ref, wu_ref, wd_ref,
-    full_out, rows_out, hidden_out, delta_out, dots_out, table_out,
+    full_out, rows_out, hidden_out, delta_out, dots_out, table_out, down_out,
     raw, rows, stage_d, stage_e, full_gate, full_up, full_down, gate_val, up_val, hg_val, select,
+    down_part, down_relay, down_in,
     load_sem, raw_ss, raw_rs, e_ss, e_rs, d_ss, d_rs, tab_ss, tab_rs,
-    w_ls, wa_ss, wa_rs, wf_ss, wf_rs, out_sem,
+    w_ls, wa_ss, wa_rs, wf_ss, wf_rs, out_sem, relay_ss, relay_rs, pair_ss, pair_rs,
 ):
     chain = Chain()
     g, me, c, z = chain.g, chain.me, chain.c, chain.z
@@ -85,18 +88,19 @@
     fulls = (full_gate, full_up, full_down)
     shards = (wg_ref, wu_ref, wd_ref)
 
-    def load(k):
-        source = tokens_ref if k < groups else grads_ref
-        return pltpu.make_async_copy(
-            source.at[:, pl.ds((k % groups) * width, width)], raw.at[0, k], load_sem.at[k]
-        )
-
-    for k in range(steps):
-        load(k).start()
+    sub = width // groups
+    for k in range(groups):
+        pltpu.make_async_copy(
+            tokens_ref.at[:, pl.ds(k * width, width)], raw.at[0, k], load_sem.at[k]
+        ).start()
+    for i in range(groups):
+        for owner in range(groups):
+            pltpu.make_async_copy(
+                grads_ref.at[:, pl.ds(owner * width + i * sub, sub)],
+                raw.at[0, groups + i, :, pl.ds(owner * sub, sub)], load_sem.at[groups + i],
+            ).start()
     for w in range(3):
         pltpu.make_async_copy(shards[w].at[0], fulls[w].at[g], w_ls.at[w]).start()
-
-    greet(chain, ranks, groups)
 
     def shard_to(w, way):
         device = (along_x, me) if way == 0 else (along_y, me)
@@ -109,38 +113,26 @@
         piece = fulls[w].at[owner, pl.ds(way * half, half)]
         return send(piece, piece, wf_ss.at[w, way], wf_rs.at[w, way], device)
 
-    for w in range(3):
-        for way in range(2):
-            shard_to(w, way).start()
-
-    experts = lax.broadcasted_iota(jnp.int32, (ranks, count), 0)
-    named = [experts == ids_ref[k : k + 1, :] for k in range(ids_ref.shape[0])]
-    hits = functools.reduce(jnp.logical_or, named)
-    before = lax.broadcasted_iota(jnp.int32, (count, count), 0) < lax.broadcasted_iota(
-        jnp.int32, (count, count), 1
-    )
-    order = dot(hits.astype(F32).astype(BF16), before.astype(F32).astype(BF16))
-    table_out[0, 0:ranks, :] = jnp.where(hits, order, -1.0)
-    weight = jnp.zeros((ranks, count), F32)
-    for k in range(ids_ref.shape[0]):
-        weight = jnp.where(named[k], weight_ref[k : k + 1, :], weight)
-    table_out[0, ranks : 2 * ranks, :] = weight
-
-    rows[:, :, cap:, :] = jnp.zeros((steps, ranks, slot_rows - cap, width), BF16)
+    def build_table():
+        experts = lax.broadcasted_iota(jnp.int32, (ranks, count), 0)
+        named = [experts == ids_ref[k : k + 1, :] for k in range(ids_ref.shape[0])]
+        hits = functools.reduce(jnp.logical_or, named)
+        before = lax.broadcasted_iota(jnp.int32, (count, count), 0) < lax.broadcasted_iota(
+            jnp.int32, (count, count), 1
+        )
+        order = dot(hits.astype(F32).astype(BF16), before.astype(F32).astype(BF16))
+        table_out[0, 0:ranks, :] = jnp.where(hits, order, -1.0)
+        weight = jnp.zeros((ranks, count), F32)
+        for k in range(ids_ref.shape[0]):
+            weight = jnp.where(named[k], weight_ref[k : k + 1, :], weight)
+        table_out[0, ranks : 2 * ranks, :] = weight
+
+        rows[:, :, cap:, :] = jnp.zeros((steps, ranks, slot_rows - cap, width), BF16)
 
     def table_send(slot, sem, zz):
         return send(
             table_out.at[0], table_out.at[slot], tab_ss.at[sem], tab_rs.at[slot - 1], chain.at(zz, c)
         )
-
-    @pl.when(is_end)
-    def _():
-        table_send(1, 0, chain.z_mid).start()
-        table_send(3, 1, chain.z_far_mid).start()
-
-    @pl.when(is_mid)
-    def _():
-        table_send(2, 0, chain.z_far_mid).start()
 
     targets = (me, me + 1 - 2 * c, 2 * chain.z_near, 2 * chain.z_near + 1)
 
@@ -154,8 +146,6 @@
                 hit, table_out[j, pl.ds(ranks + rank, 1), :], 0.0
             ).astype(BF16)
 
-    selectors(0)
-
     def gather(j, k, z_from, blocks, e_slot):
         picked = dot(select[k // groups, j, 0 : blocks * slot_rows, :], raw[j, k]).astype(BF16)
         parts = [picked[i * slot_rows : (i + 1) * slot_rows] for i in range(blocks)]
@@ -165,6 +155,7 @@
             stage_e[k, i - 2, e_slot] = parts[i]
 
     full = pl.ds(0, cap)
+    far_places = ((chain.z_far_mid, 1), (chain.z_far_end, 2))
 
     def own_raw(k):
         return send(raw.at[0, k], raw.at[2, k], raw_ss.at[0, k], raw_rs.at[1, k], chain.at(chain.z_far_mid, c))
@@ -181,10 +172,11 @@
             e_ss.at[k, 0, i], e_rs.at[k, 0, c], chain.at(chain.z_end, i),
         )
 
-    def far_to_end(k, i):
-        return send(
-            stage_e.at[k, i, pl.ds(1, 2), full], rows.at[k, pl.ds(4 * c + 2 * chain.far, 2), full],
-            e_ss.at[k, 1, i], e_rs.at[k, 1, c], chain.at(chain.z_end, i),
+    def far_to_end(k, i, which):
+        z_from, slot = far_places[which]
+        return send(
+            stage_e.at[k, i, slot, full], rows.at[k, 4 * c + z_from, full],
+            e_ss.at[k, 1 + which, i], e_rs.at[k, 1 + which, c], chain.at(chain.z_end, i),
         )
 
     def mid_to_partner(k):
@@ -203,10 +195,10 @@
             e_ss.at[k, 0, 0], e_rs.at[k, 0, core], chain.at(chain.z_mid, core),
         )
 
-    def far_blocks_from(k, core):
-        return send(
-            stage_e.at[k, 0, pl.ds(1, 2), full], rows.at[k, pl.ds(4 * core + 2 * chain.far, 2), full],
-            e_ss.at[k, 1, 0], e_rs.at[k, 1, core], chain.at(chain.z_mid, core),
+    def far_block_from(k, core, which):
+        return send(
+            stage_e.at[k, 0, 1, full], rows.at[k, 4 * core + far_places[which][0], full],
+            e_ss.at[k, 1 + which, 0], e_rs.at[k, 1 + which, core], chain.at(chain.z_mid, core),
         )
 
     def landed(k):
@@ -219,21 +211,140 @@
             end_to_partner(k).wait_recv()
             for core in range(2):
                 own_block_from(k, core).wait_recv()
-                far_blocks_from(k, core).wait_recv()
+                for which in range(2):
+                    far_block_from(k, core, which).wait_recv()
 
     def load_wait(k):
         pltpu.make_async_copy(
             tokens_ref.at[:, pl.ds(0, width)], raw.at[0, k], load_sem.at[k]
         ).wait()
 
+    across = groups - 1 - g
+    slots = ranks * slot_rows
+    half_inner = hidden_out.shape[2] // 2
+
+    def hidden_grad(q, carry):
+        landed(groups + q)
+
+        def tile(t, carry):
+            four = pl.ds(4 * t, 4)
+            value = functools.reduce(jnp.add, [
+                dot(
+                    rows[groups + q, four, :, owner * sub : (owner + 1) * sub].reshape(4 * slot_rows, sub),
+                    full_down[owner, :, pl.ds(pl.multiple_of(q * sub, 128), sub)], 1, 1,
+                )
+                for owner in range(groups)
+            ]).reshape(4, slot_rows, hg_val.shape[2])
+
+            @pl.when(q == 0)
+            def _():
+                hg_val[four] = value
+
+            @pl.when(q > 0)
+            def _():
+                hg_val[four] += value
+
+            return carry
+
+        return lax.fori_loop(0, ranks // 4, tile, carry)
+
+    def block_of(tile):
+        return pl.ds(tile * half_inner, half_inner)
+
+    def of_owner(owner):
+        return pl.ds(pl.multiple_of(owner * sub, 128), sub)
+
+    def relay_to(i, way):
+        device = (along_x, me) if way == 0 else (along_y, me)
+        return send(
+            down_part.at[i, block_of(way), of_owner(across)], down_relay.at[i, way],
+            relay_ss.at[i, way], relay_rs.at[i, way], device,
+        )
+
+    def pair_to(i, way):
+        owner = along_x if way == 0 else along_y
+        return send(
+            down_part.at[i, :, of_owner(owner)], down_in.at[i, way],
+            pair_ss.at[i, way], pair_rs.at[i, way], (owner, me),
+        )
+
+    def down_make(i):
+        for tile in range(2):
+            left = hidden_out[:, :, tile * half_inner : (tile + 1) * half_inner].reshape(slots, half_inner)
+            down_part[i, block_of(tile), :] = dot(
+                left, rows[groups + i].reshape(slots, width), 0, 0
+            ).astype(BF16)
+        for way in range(2):
+            relay_to(i, way).start()
+
+    def down_pass(i):
+        for way in range(2):
+            owner = along_x if way == 0 else along_y
+            relay_to(i, 1 - way).wait_recv()
+            place = (i, block_of(1 - way), of_owner(owner))
+            down_part[place] = (
+                down_part[place].astype(F32) + down_relay[i, 1 - way].astype(F32)
+            ).astype(BF16)
+            pair_to(i, way).start()
+
+    def down_own(i):
+        for way in range(2):
+            pair_to(i, way).wait_recv()
+        total = down_part[i, :, of_owner(g)].astype(F32)
+        for way in range(2):
+            total = total + down_in[i, way].astype(F32)
+        down_out[:, of_owner(i)] = total.astype(BF16)
+
+    ahead = 2
+
+    def prologue():
+        build_table()
+        selectors(0)
+        for k in range(ahead):
+            load_wait(k)
+
+            @pl.when(is_mid)
+            def _():
+                gather(0, k, z, 4, 0)
+
+    greet(chain, ranks, groups, prologue)
+    for way in range(2):
+        shard_to(0, way).start()
+
+    @pl.when(is_mid)
+    def _():
+        own_raw(0).start()
+        for k in range(ahead):
+            own_to_end(k, 0).start()
+            own_to_end(k, 1).start()
+
+    @pl.when(is_end)
+    def _():
+        end_raw(0).start()
+        table_send(1, 0, chain.z_mid).start()
+        table_send(3, 1, chain.z_far_mid).start()
+
+    @pl.when(is_mid)
+    def _():
+        table_send(2, 0, chain.z_far_mid).start()
+
+    for w in range(1, 3):
+        for way in range(2):
+            shard_to(w, way).start()
+    for k in range(ahead, steps):
+        load_wait(k)
+
+    @pl.when(is_end)
+    def _():
+        for k in range(1, steps):
+            end_raw(k).start()
+
     def step(k, carry):
         @pl.when(is_mid & (k < steps))
         def _():
-            load_wait(k)
-            own_raw(k).start()
-            gather(0, k, z, 4, 0)
-            own_to_end(k, 0).start()
-            own_to_end(k, 1).start()
+            @pl.when(k > 0)
+            def _():
+                own_raw(k).start()
 
             @pl.when(k == 0)
             def _():
@@ -242,6 +353,13 @@
 
             end_raw(k).wait_recv()
             onward_raw(k).start()
+
+            @pl.when(k + ahead < steps)
+            def _():
+                gather(0, k + ahead, z, 4, 0)
+                own_to_end(k + ahead, 0).start()
+                own_to_end(k + ahead, 1).start()
+
             gather(1, k, chain.z_end, 2, 0)
 
         @pl.when(is_mid & (k >= 1))
@@ -255,22 +373,22 @@
 
             j = k - 1
             own_raw(j).wait_recv()
-            gather(2, j, chain.z_far_mid, 4, 1 + chain.half)
+            gather(2, j, chain.z_far_mid, 4, 1)
+            far_to_end(j, 0, 0).start()
+            far_to_end(j, 1, 0).start()
             onward_raw(j).wait_recv()
-            gather(3, j, chain.z_far_end, 4, 1 + chain.far)
-            far_to_end(j, 0).start()
-            far_to_end(j, 1).start()
+            gather(3, j, chain.z_far_end, 4, 2)
+            far_to_end(j, 0, 1).start()
+            far_to_end(j, 1, 1).start()
             mid_to_partner(j).start()
 
         @pl.when(is_end & (k < steps))
         def _():
-            load_wait(k)
-            end_raw(k).start()
             gather(0, k, z, 2, 0)
             end_to_partner(k).start()
 
         for w in range(3):
-            @pl.when(k == w + 1)
+            @pl.when(k == w + 2)
             def _():
                 for way in range(2):
                     shard_to(w, 1 - way).wait_recv()
@@ -285,16 +403,38 @@
                 for way in range(2):
                     forward_half(w, way).wait_recv()
 
-        @pl.when(k >= groups + 1)
-        def _():
-            pair = pl.ds(2 * (k - groups - 1), 2)
-            shape = (2, slot_rows, gate_val.shape[2])
-            piece = [rows[kk, pair].reshape(2 * slot_rows, width) for kk in range(groups)]
-            gate = functools.reduce(jnp.add, [dot(piece[kk], full_gate[kk]) for kk in range(groups)])
-            up = functools.reduce(jnp.add, [dot(piece[kk], full_up[kk]) for kk in range(groups)])
-            gate_val[pair] = gate.reshape(shape)
-            up_val[pair] = up.reshape(shape)
-            hidden_out[pair] = (gate * jax.nn.sigmoid(gate) * up).astype(BF16).reshape(shape)
+        @pl.when((k == groups + 1) | (k == groups + 2))
+        def _():
+            def forward(p, carry):
+                pair = pl.ds(2 * p, 2)
+                shape = (2, slot_rows, gate_val.shape[2])
+                piece = [rows[kk, pair].reshape(2 * slot_rows, width) for kk in range(groups)]
+                gate = functools.reduce(jnp.add, [dot(piece[kk], full_gate[kk]) for kk in range(groups)])
+                up = functools.reduce(jnp.add, [dot(piece[kk], full_up[kk]) for kk in range(groups)])
+                gate_val[pair] = gate.reshape(shape)
+                up_val[pair] = up.reshape(shape)
+                hidden_out[pair] = (gate * jax.nn.sigmoid(gate) * up).astype(BF16).reshape(shape)
+                return carry
+
+            start = (k - groups - 1) * (ranks // 4)
+            lax.fori_loop(start, start + ranks // 4, forward, 0)
+
+        @pl.when(k == groups + 2)
+        def _():
+            pltpu.make_async_copy(shards[2].at[0], fulls[2].at[g], w_ls.at[2]).wait()
+            for way in range(2):
+                forward_half(2, way).wait_recv()
+
+        @pl.when(k >= groups + 2)
+        def _():
+            q = k - groups - 2
+
+            @pl.when(q >= 1)
+            def _():
+                down_pass(q - 1)
+
+            hidden_grad(q, 0)
+            down_make(q)
 
         return carry
 
@@ -309,32 +449,10 @@
     first = pltpu.make_async_copy(rows.at[pl.ds(0, groups)], rows_out.at[pl.ds(0, groups)], out_sem.at[2])
     first.start()
 
-    pltpu.make_async_copy(shards[2].at[0], fulls[2].at[g], w_ls.at[2]).wait()
-    for way in range(2):
-        forward_half(2, way).wait_recv()
-
-    def hidden_grad(q, carry):
-        landed(groups + q)
-        pltpu.make_async_copy(rows.at[groups + q], rows_out.at[groups + q], out_sem.at[3 + q]).start()
-
-        def tile(t, carry):
-            four = pl.ds(4 * t, 4)
-            left = rows[groups + q, four].reshape(4 * slot_rows, width)
-            value = dot(left, full_down[q], 1, 1).reshape(4, slot_rows, hg_val.shape[2])
-
-            @pl.when(q == 0)
-            def _():
-                hg_val[four] = value
-
-            @pl.when(q > 0)
-            def _():
-                hg_val[four] += value
-
-            return carry
-
-        return lax.fori_loop(0, ranks // 4, tile, carry)
-
-    lax.fori_loop(0, groups, hidden_grad, 0)
+    down_pass(groups - 2)
+    hidden_grad(groups - 1, 0)
+    late = pltpu.make_async_copy(rows.at[steps - 1], rows_out.at[groups], out_sem.at[3])
+    late.start()
 
     def deltas(t, carry):
         gate, up, grad = gate_val[t], up_val[t], hg_val[t]
@@ -350,8 +468,16 @@
     for copy in outs:
         copy.wait()
     first.wait()
-    for q in range(groups):
-        pltpu.make_async_copy(rows.at[groups + q], rows_out.at[groups + q], out_sem.at[3 + q]).wait()
+    late.wait()
+
+    def finish_down(i, carry):
+        down_own(i)
+        for way in range(2):
+            relay_to(i, way).wait_send()
+            pair_to(i, way).wait_send()
+        return carry
+
+    lax.fori_loop(0, groups - 1, finish_down, 0)
     for w in range(3):
         for way in range(2):
             shard_to(w, way).wait_send()
@@ -364,7 +490,8 @@
             onward_raw(k).wait_send()
             for i in range(2):
                 own_to_end(k, i).wait_send()
-                far_to_end(k, i).wait_send()
+                for which in range(2):
+                    far_to_end(k, i, which).wait_send()
             mid_to_partner(k).wait_send()
 
         @pl.when(is_end)
@@ -400,14 +527,15 @@
         functools.partial(forward_kernel, cap),
         out_shape=(
             jax.ShapeDtypeStruct((2, groups, width, inner), BF16),
-            jax.ShapeDtypeStruct((steps, ranks, slot_rows, width), BF16),
+            jax.ShapeDtypeStruct((groups + 1, ranks, slot_rows, width), BF16),
             jax.ShapeDtypeStruct((ranks, slot_rows, inner), BF16),
             jax.ShapeDtypeStruct((2, ranks, slot_rows, inner), BF16),
             jax.ShapeDtypeStruct((ranks, 8, slot_rows), F32),
             jax.ShapeDtypeStruct((4, 2 * ranks, count), F32),
+            jax.ShapeDtypeStruct((inner, width), BF16),
         ),
         in_specs=[vmem, vmem, hbm, hbm, hbm, hbm, hbm],
-        out_specs=(hbm, hbm, vmem, vmem, vmem, vmem),
+        out_specs=(hbm, hbm, vmem, vmem, vmem, vmem, vmem),
         scratch_shapes=[
             pltpu.VMEM((4, steps, count, width), BF16),
             pltpu.VMEM((steps, ranks, slot_rows, width), BF16),
@@ -420,9 +548,13 @@
             pltpu.VMEM((ranks, slot_rows, inner), F32),
             pltpu.VMEM((ranks, slot_rows, inner), F32),
             pltpu.VMEM((2, 4, 4 * slot_rows, count), BF16),
-            dma((steps,)), dma((2, steps)), dma((3, steps)), dma((steps, 2, 2)), dma((steps, 2, 2)),
+            pltpu.VMEM((groups - 1, inner, width), BF16),
+            pltpu.VMEM((groups - 1, 2, inner // 2, width // groups), BF16),
+            pltpu.VMEM((groups - 1, 2, inner, width // groups), BF16),
+            dma((steps,)), dma((2, steps)), dma((3, steps)), dma((steps, 3, 2)), dma((steps, 3, 2)),
             dma((steps,)), dma((steps,)), dma((2,)), dma((3,)),
-            dma((3,)), dma((3, 2)), dma((3, 2)), dma((3, 2)), dma((3, 2)), dma((3 + groups,)),
+            dma((3,)), dma((3, 2)), dma((3, 2)), dma((3, 2)), dma((3, 2)), dma((4,)),
+            dma((groups - 1, 2)), dma((groups - 1, 2)), dma((groups - 1, 2)), dma((groups - 1, 2)),
         ],
         compiler_params=pltpu.CompilerParams(
             collective_id=0, has_side_effects=True, vmem_limit_bytes=67000000
@@ -432,10 +564,10 @@
 
 def backward_kernel(
     cap,
-    ids_ref, weight_ref, table_ref, dots_ref, full_ref, rows_ref, hidden_ref, delta_ref,
+    ids_ref, weight_ref, table_ref, dots_ref, full_ref, rows_ref, hidden_ref, delta_ref, down_ref,
     token_out, route_out, gate_out, up_out, down_out,
     full, rows, hidden, delta, grads, comb, gf_send, gf_in, end_send, select,
-    diag_gu, diag_d, pair_gu, pair_d, relay_gu, relay_d, in_gu, in_d, dots_in,
+    diag_gu, pair_gu, pair_d, relay_gu, relay_d, in_gu, in_d, dots_in,
     load_sem, d_ss, d_rs, far_ss, far_rs, near_ss, near_rs, gf_ss, gf_rs, es_ss, es_rs,
     dots_ss, dots_rs, relay_ss, relay_rs, pair_ss, pair_rs,
 ):
@@ -450,22 +582,27 @@
     along_x, along_y = neighbours(g)
     across = groups - 1 - g
     slots = ranks * slot_rows
+    subs, narrow = grads.shape[0], grads.shape[3]
 
     loads = [
         pltpu.make_async_copy(delta_ref, delta, load_sem.at[0]),
-        pltpu.make_async_copy(rows_ref.at[across], rows.at[across], load_sem.at[1]),
-        pltpu.make_async_copy(full_ref.at[:, 0], full.at[:, 0], load_sem.at[2]),
-        pltpu.make_async_copy(hidden_ref, hidden, load_sem.at[3]),
-        pltpu.make_async_copy(rows_ref.at[groups + across], rows.at[groups + across], load_sem.at[4]),
-        pltpu.make_async_copy(full_ref.at[:, pl.ds(1, groups - 1)], full.at[:, pl.ds(1, groups - 1)], load_sem.at[5]),
+        pltpu.make_async_copy(full_ref.at[:, 0], full.at[:, 0], load_sem.at[1]),
+        pltpu.make_async_copy(rows_ref.at[across], rows.at[across], load_sem.at[2]),
+        pltpu.make_async_copy(full_ref.at[:, pl.ds(1, subs - 1)], full.at[:, pl.ds(1, subs - 1)], load_sem.at[3]),
+        pltpu.make_async_copy(rows_ref.at[groups], rows.at[groups], load_sem.at[4]),
+        pltpu.make_async_copy(hidden_ref, hidden, load_sem.at[5]),
     ]
     for i, shard in enumerate((along_x, along_y, g)):
         loads.append(pltpu.make_async_copy(rows_ref.at[shard], rows.at[shard], load_sem.at[6 + i]))
-        loads.append(
-            pltpu.make_async_copy(rows_ref.at[groups + shard], rows.at[groups + shard], load_sem.at[9 + i])
-        )
     for copy in loads:
         copy.start()
+    sub = width // groups
+    half_inner = inner // 2
+    down_ready = pltpu.make_async_copy(down_ref, down_out, load_sem.at[9])
+    down_ready.start()
+
+    def of_owner(owner):
+        return pl.ds(pl.multiple_of(owner * sub, 128), sub)
 
     greet(chain, ranks, groups)
 
@@ -485,7 +622,7 @@
     for step in range(1, ranks):
         dots_to((me + step) % ranks).start()
 
-    comb[:, :, :, cap:, :] = jnp.zeros((groups, 4, 4, slot_rows - cap, width), BF16)
+    comb[:, :, :, cap:, :] = jnp.zeros((subs, 4, 4, slot_rows - cap, narrow), BF16)
     targets = (me, me + 1 - 2 * c, 2 * chain.z_near, 2 * chain.z_near + 1)
 
     def selectors(j, z_from):
@@ -540,8 +677,10 @@
             near_ss.at[k, core], near_rs.at[k, core], chain.at(chain.z_end, core),
         )
 
-    def sums_across(k):
-        return send(gf_send.at[k], gf_in.at[k], gf_ss.at[k], gf_rs.at[k], chain.at(chain.z_far_mid, c))
+    def sums_across(k, home):
+        return send(
+            gf_send.at[k, home], gf_in.at[k, home], gf_ss.at[k, home], gf_rs.at[k, home], chain.at(chain.z_far_mid, c)
+        )
 
     def sums_to_end(k):
         return send(end_send.at[k], gf_in.at[k, 0], es_ss.at[k], es_rs.at[k], chain.at(chain.z_end, c))
@@ -551,40 +690,35 @@
 
     def relay_to(w, way):
         if w == 2:
-            half = diag_d.shape[0] // 2
-            src, dst = diag_d.at[pl.ds(way * half, half)], relay_d.at[way]
+            src, dst = pair_d.at[pl.ds(way * half_inner, half_inner), of_owner(across)], relay_d.at[way]
         else:
-            half = diag_gu.shape[1] // 2
+            half = width // 2
             src, dst = diag_gu.at[w, pl.ds(way * half, half)], relay_gu.at[w, way]
         return send(src, dst, relay_ss.at[w, way], relay_rs.at[w, way], device_on(way))
 
     def pair_to(w, way):
-        src, dst = (pair_d.at[way], in_d.at[way]) if w == 2 else (pair_gu.at[w, way], in_gu.at[w, way])
+        if w == 2:
+            src, dst = pair_d.at[:, of_owner(along_x if way == 0 else along_y)], in_d.at[way]
+        else:
+            src, dst = pair_gu.at[w, way], in_gu.at[w, way]
         return send(src, dst, pair_ss.at[w, way], pair_rs.at[w, way], device_on(way))
 
     def part(w, shard, tile):
+        half = width // 2
+        left = rows[shard, :, :, tile * half : (tile + 1) * half].reshape(slots, half)
+        return dot(left, delta[w].reshape(slots, inner), 0, 0)
+
+    def diagonal(w):
         if w == 2:
-            half = inner // 2
-            left = hidden[:, :, pl.ds(tile * half, half)].reshape(slots, half)
-            return dot(left, rows[groups + shard].reshape(slots, width), 0, 0)
-        half = width // 2
-        left = rows[shard, :, :, pl.ds(tile * half, half)].reshape(slots, half)
-        return dot(left, delta[w].reshape(slots, inner), 0, 0)
-
-    def over_two(body):
-        for tile in range(2):
-            body(tile)
-
-    def diagonal(w):
-        def body(tile):
-            value = part(w, across, tile).astype(BF16)
-            half = value.shape[0]
-            if w == 2:
-                diag_d[pl.ds(tile * half, half), :] = value
-            else:
-                diag_gu[w, pl.ds(tile * half, half), :] = value
-
-        over_two(body)
+            for tile in range(2):
+                left = hidden[:, :, tile * half_inner : (tile + 1) * half_inner].reshape(slots, half_inner)
+                pair_d[pl.ds(tile * half_inner, half_inner), :] = dot(
+                    left, rows[groups].reshape(slots, width), 0, 0
+                ).astype(BF16)
+        else:
+            half = width // 2
+            for tile in range(2):
+                diag_gu[w, pl.ds(tile * half, half), :] = part(w, across, tile).astype(BF16)
         for way in range(2):
             relay_to(w, way).start()
 
@@ -592,42 +726,41 @@
         for way in range(2):
             shard = along_x if way == 0 else along_y
             relay_to(w, 1 - way).wait_recv()
-
-            def body(tile):
-                value = part(w, shard, tile)
-                half = value.shape[0]
-                if tile == 1 - way:
-                    come = relay_d[1 - way] if w == 2 else relay_gu[w, 1 - way]
-                    value = value.astype(BF16).astype(F32) + come.astype(F32)
-                value = value.astype(BF16)
-                if w == 2:
-                    pair_d[way, pl.ds(tile * half, half), :] = value
-                else:
+            if w == 2:
+                place = (pl.ds((1 - way) * half_inner, half_inner), of_owner(shard))
+                pair_d[place] = (pair_d[place].astype(F32) + relay_d[1 - way].astype(F32)).astype(BF16)
+            else:
+                half = width // 2
+                for tile in range(2):
+                    value = part(w, shard, tile).astype(BF16)
+                    if tile == 1 - way:
+                        value = (value.astype(F32) + relay_gu[w, 1 - way].astype(F32)).astype(BF16)
                     pair_gu[w, way, pl.ds(tile * half, half), :] = value
-
-            over_two(body)
             pair_to(w, way).start()
 
     def finish(w):
         for way in range(2):
             pair_to(w, way).wait_recv()
-
-        def body(tile):
-            value = part(w, g, tile)
-            half = value.shape[0]
-            block = pl.ds(tile * half, half)
+        if w == 2:
+            total = pair_d[:, of_owner(g)].astype(F32)
             for way in range(2):
-                come = in_d[way, block, :] if w == 2 else in_gu[w, way, block, :]
-                value = value + come.astype(F32)
-            (gate_out, up_out, down_out)[w][block, :] = value.astype(BF16)
-
-        over_two(body)
+                total = total + in_d[way].astype(F32)
+            down_ready.wait()
+            down_out[:, of_owner(groups - 1)] = total.astype(BF16)
+        else:
+            half = width // 2
+            for tile in range(2):
+                value = part(w, g, tile)
+                block = pl.ds(tile * half, half)
+                for way in range(2):
+                    value = value + in_gu[w, way, block, :].astype(F32)
+                (gate_out, up_out)[w][block, :] = value.astype(BF16)
 
     def input_grad(k):
         for hc in range(2):
             left = [delta[w, pl.ds(4 * hc, 4)].reshape(4 * slot_rows, inner) for w in range(2)]
             value = (dot(left[0], full[0, k], 1, 1) + dot(left[1], full[1, k], 1, 1)).astype(BF16)
-            value = value.reshape(4, slot_rows, width)
+            value = value.reshape(4, slot_rows, narrow)
             grads[k, pl.ds(4 * hc, 4)] = value
 
             @pl.when(c == hc)
@@ -637,68 +770,84 @@
     def summed(k, z_from, blocks):
         return dot(
             select[z_from, 0 : blocks * slot_rows, :],
-            comb[k, z_from, 0:blocks].reshape(blocks * slot_rows, width), 0, 0,
-        )
-
-    for i in range(3):
+            comb[k, z_from, 0:blocks].reshape(blocks * slot_rows, narrow), 0, 0,
+        )
+
+    for i in range(2):
         loads[i].wait()
 
-    def first(k, carry):
-        for w in range(3):
+    lag = 2
+
+    def along(k, carry):
+        @pl.when(k == 1)
+        def _():
+            loads[3].wait()
+
+        @pl.when(k < subs)
+        def _():
+            input_grad(k)
+
+            @pl.when(is_mid)
+            def _():
+                to_partner(k).start()
+
+            @pl.when(is_end)
+            def _():
+                for core in range(2):
+                    far_home(k, core).start()
+                end_to_partner(k).start()
+
+        @pl.when(is_end & (k == subs - 1))
+        def _():
+            for j in range(subs):
+                for core in range(2):
+                    near_home(j, core).start()
+
+        for w in range(2):
             @pl.when(k == w)
             def _():
-                if w == 2:
-                    loads[3].wait()
-                    loads[4].wait()
+                if w == 0:
+                    loads[2].wait()
                 diagonal(w)
 
-        @pl.when(k == 1)
-        def _():
+        @pl.when(k == 2)
+        def _():
+            loads[4].wait()
             loads[5].wait()
 
-        input_grad(k)
-
-        @pl.when(is_mid)
-        def _():
-            to_partner(k).start()
-
-        @pl.when(is_end)
-        def _():
+            diagonal(2)
+
+        @pl.when(is_mid & (k >= 1) & (k <= subs))
+        def _():
+            j = k - 1
+            to_partner(j).wait_recv()
             for core in range(2):
-                far_home(k, core).start()
-            end_to_partner(k).start()
+                far_from(j, core).wait_recv()
+            gf_send[j, 1] = summed(j, chain.z_far_end, 4).astype(BF16)
+            sums_across(j, 1).start()
+            gf_send[j, 0] = summed(j, chain.z_far_mid, 4).astype(BF16)
+            sums_across(j, 0).start()
+
+        @pl.when(k == 3)
+        def _():
+            for copy in loads[6:]:
+                copy.wait()
+
+        for at, w in ((3, 0), (4, 2), (5, 1)):
+            @pl.when(k == at)
+            def _():
+                pairs(w)
+
+        @pl.when(is_mid & (k > lag))
+        def _():
+            j = k - 1 - lag
+            sums_across(j, 1).wait_recv()
+            end_send[j] = (summed(j, chain.z_end, 2) + gf_in[j, 1].astype(F32)).astype(BF16)
+            sums_to_end(j).start()
 
         return carry
 
-    lax.fori_loop(0, groups, first, 0)
-
-    @pl.when(is_end)
-    def _():
-        for k in range(groups):
-            for core in range(2):
-                near_home(k, core).start()
-
-    for copy in loads[6:]:
-        copy.wait()
-
-    def second(k, carry):
-        for w in range(3):
-            @pl.when(k == w)
-            def _():
-                pairs(w)
-
-        @pl.when(is_mid)
-        def _():
-            to_partner(k).wait_recv()
-            for core in range(2):
-                far_from(k, core).wait_recv()
-            gf_send[k, 0] = summed(k, chain.z_far_mid, 4).astype(BF16)
-            gf_send[k, 1] = summed(k, chain.z_far_end, 4).astype(BF16)
-            sums_across(k).start()
-
-        return carry
-
-    lax.fori_loop(0, groups, second, 0)
+    lax.fori_loop(0, subs + 1 + lag, along, 0)
 
     for step in range(1, ranks):
         dots_from((me + step) % ranks).wait_recv()
@@ -715,22 +864,23 @@
     route_out[...] = found / weight_ref[...]
 
     def third(k, carry):
-        columns = pl.ds(pl.multiple_of(k * width, 128), width)
+        columns = pl.ds(pl.multiple_of(k * narrow, 128), narrow)
+
+        @pl.when(k == 0)
+        def _():
+            finish(0)
+
+        @pl.when(k == 3)
+        def _():
+            finish(2)
 
         @pl.when(is_mid)
         def _():
-            sums_across(k).wait_recv()
-            end_send[k] = (summed(k, chain.z_end, 2) + gf_in[k, 1].astype(F32)).astype(BF16)
-            sums_to_end(k).start()
+            sums_across(k, 0).wait_recv()
             for core in range(2):
                 near_from(k, core).wait_recv()
             token_out[:, columns] = (summed(k, z, 4) + gf_in[k, 0].astype(F32)).astype(BF16)
 
-        for w in range(3):
-            @pl.when(k == w + 1)
-            def _():
-                finish(w)
-
         @pl.when(is_end)
         def _():
             end_to_partner(k).wait_recv()
@@ -739,8 +889,9 @@
 
         return carry
 
-    lax.fori_loop(0, groups, third, 0)
-
+    lax.fori_loop(0, subs, third, 0)
+
+    finish(1)
     for w in range(3):
         for way in range(2):
             relay_to(w, way).wait_send()
@@ -752,7 +903,8 @@
         @pl.when(is_mid)
         def _():
             to_partner(k).wait_send()
-            sums_across(k).wait_send()
+            for home in range(2):
+                sums_across(k, home).wait_send()
             sums_to_end(k).wait_send()
 
         @pl.when(is_end)
@@ -764,14 +916,16 @@
 
         return carry
 
-    lax.fori_loop(0, groups, drain, 0)
-
-
-def backward_call(ids_t, weight_t, table, dots, full, rows, hidden, delta, cap):
+    lax.fori_loop(0, subs, drain, 0)
+
+
+def backward_call(ids_t, weight_t, table, dots, full, rows, hidden, delta, down, cap):
     groups, ranks = lax.axis_size("dp"), lax.axis_size("expert")
     _, _, slot_rows, width = rows.shape
     count = table.shape[2]
     inner = hidden.shape[2]
+    subs, narrow = 2 * groups, width // 2
+    full = full.reshape(2, subs, narrow, inner)
     hbm = pl.BlockSpec(memory_space=pl.ANY)
     vmem = pl.BlockSpec(memory_space=pltpu.VMEM)
     dma = pltpu.SemaphoreType.DMA
@@ -784,36 +938,35 @@
             jax.ShapeDtypeStruct((width, inner), BF16),
             jax.ShapeDtypeStruct((inner, width), BF16),
         ),
-        in_specs=[vmem, vmem, vmem, vmem, hbm, hbm, hbm, hbm],
+        in_specs=[vmem, vmem, vmem, vmem, hbm, hbm, hbm, hbm, hbm],
         out_specs=(vmem,) * 5,
         scratch_shapes=[
             pltpu.VMEM(full.shape, BF16),
             pltpu.VMEM(rows.shape, BF16),
             pltpu.VMEM(hidden.shape, BF16),
             pltpu.VMEM(delta.shape, BF16),
-            pltpu.VMEM((groups, ranks, slot_rows, width), BF16),
-            pltpu.VMEM((groups, 4, 4, slot_rows, width), BF16),
-            pltpu.VMEM((groups, 2, count, width), BF16),
-            pltpu.VMEM((groups, 2, count, width), BF16),
-            pltpu.VMEM((groups, count, width), BF16),
+            pltpu.VMEM((subs, ranks, slot_rows, narrow), BF16),
+            pltpu.VMEM((subs, 4, 4, slot_rows, narrow), BF16),
+            pltpu.VMEM((subs, 2, count, narrow), BF16),
+            pltpu.VMEM((subs, 2, count, narrow), BF16),
+            pltpu.VMEM((subs, count, narrow), BF16),
             pltpu.VMEM((4, 4 * slot_rows, count), BF16),
             pltpu.VMEM((2, width, inner), BF16),
+            pltpu.VMEM((2, 2, width, inner), BF16),
             pltpu.VMEM((inner, width), BF16),
+            pltpu.VMEM((2, 2, width // 2, inner), BF16),
+            pltpu.VMEM((2, inner // 2, width // groups), BF16),
             pltpu.VMEM((2, 2, width, inner), BF16),
-            pltpu.VMEM((2, inner, width), BF16),
-            pltpu.VMEM((2, 2, width // 2, inner), BF16),
-            pltpu.VMEM((2, inner // 2, width), BF16),
-            pltpu.VMEM((2, 2, width, inner), BF16),
-            pltpu.VMEM((2, inner, width), BF16),
+            pltpu.VMEM((2, inner, width // groups), BF16),
             pltpu.VMEM(dots.shape, F32),
-            dma((12,)), dma((groups,)), dma((groups,)), dma((groups, 2)), dma((groups, 2)),
-            dma((groups, 2)), dma((groups, 2)), dma((groups,)), dma((groups,)), dma((groups,)), dma((groups,)),
+            dma((12,)), dma((subs,)), dma((subs,)), dma((subs, 2)), dma((subs, 2)),
+            dma((subs, 2)), dma((subs, 2)), dma((subs, 2)), dma((subs, 2)), dma((subs,)), dma((subs,)),
             dma((ranks,)), dma((ranks,)), dma((3, 2)), dma((3, 2)), dma((3, 2)), dma((3, 2)),
         ],
         compiler_params=pltpu.CompilerParams(
             collective_id=1, has_side_effects=True, vmem_limit_bytes=67000000
         ),
-    )(ids_t, weight_t, table, dots, full, rows, hidden, delta)
+    )(ids_t, weight_t, table, dots, full, rows, hidden, delta, down)
 
 
 def swap(block, axis, distance):
@@ -942,11 +1095,11 @@
     count = tokens.shape[0]
     cap = 3 * count * expert_ids.shape[1] // (2 * lax.axis_size("expert"))
     ids_t, weight_t = expert_ids.T, route_weight.T.astype(F32)
-    full, rows, hidden, delta, dots, table = forward_call(
+    full, rows, hidden, delta, dots, table, down = forward_call(
         ids_t, weight_t, tokens, out_grad, w_gate, w_up, w_down, cap
     )
     token_grad, route_grad, gate_grad, up_grad, down_grad = backward_call(
-        ids_t, weight_t, table, dots, full, rows, hidden, delta, cap
+        ids_t, weight_t, table, dots, full, rows, hidden, delta, down, cap
     )
     return token_grad, route_grad.T.astype(BF16), gate_grad[None], up_grad[None], down_grad[None]
 

time: 245 us -> 229 us (0.935)
  Pallas kernels: 236 us -> 220 us
    pallas_call x1, Pallas kernels: 87.6 us -> 75.9 us  [backward_call(): pl.pallas_call(functools.partial(backward_kernel, cap), out_shape=(jax.Sh...]
    pallas_call x1, Pallas kernels: 149 us -> 144 us  [forward_call(): pl.pallas_call(functools.partial(forward_kernel, cap), out_shape=(jax.Sha...]
where the time goes in v2:
time: 229 us
  Pallas kernels  220 us (96%)
  local copies, waits for them, and re-layouts  5.24 us (2%)
  other arithmetic  2.58 us (1%)
    pallas_call x1, Pallas kernels, forward_call(): pl.pallas_call(functools.partial(forward_kernel, cap), out_shape=(jax.Sha...  144 us
    pallas_call x1, Pallas kernels, backward_call(): pl.pallas_call(functools.partial(backward_kernel, cap), out_shape=(jax.Sh...  75.9 us
    unnamed x10, local copies, waits for them, and re-layouts  5.24 us

profile of v2, /device:TPU:1, one launch (start us, length us, event | category | flops | bytes accessed | tf_op | source)
XLA Modules:
  0.0 228.6 jit_solution(8146199443455562104)
XLA Ops:
  0.6 1.3 convert_bitcast_fusion.weight_ref
  1.9 144.2 %shard_map.110 = (bf16[2,4,512,768]{3,2,1,0:T(8,128)(2,1)}, bf16[5,8,128,512]{3,2,1,0:T(8,128)(2,1)}, bf16[8,128,768]{2,1,0:T(8,128)(2,1)}, bf16[2,8,128,768]{3,...) custom-call(s32[2,320]{1,0:T(2,128)} %bitcast.13, ...), custom_call_target="tpu_custom_call" | custom-call | tf_op jit(solution)/shard_map/pallas_call | solution.py:526
  146.1 75.9 %shard_map.111 = (bf16[320,2048]{1,0:T(8,128)(2,1)}, f32[2,320]{1,0:T(2,128)}, bf16[512,768]{1,0:T(8,128)(2,1)}, bf16[512,768]{1,0:T(8,128)(2,1)}, bf16[768,512]{1,0:T(8,128)(2,1)}) custom-call(s32[2,320]{1,0:T(2,128)} %bitcast.14, f32[2,320]{1,0:T(2,128)} %convert_bitcast_fusion.weight_ref, f32[4,16,320]{2,1,0:T(8,128)} %get-tuple-element.17.table_ref, ...), custom_call_target="tpu_custom_call" | custom-call | tf_op jit(solution)/shard_map/pallas_call | solution.py:932
  222.0 0.0 copy-start.2
  222.0 1.3 convert_bitcast_fusion.1
  223.3 0.0 copy-start.1
  223.3 2.6 %copy.16 = bf16[320,2048]{1,0:T(8,128)(2,1)} copy(bf16[320,2048]{1,0:T(8,128)(2,1)} %get-tuple-element.34) | data formatting | bytes 2621440
  225.9 0.0 copy-done.2
  225.9 0.0 copy-start
  225.9 0.9 copy.17
  226.8 0.0 copy-done.1
  226.8 0.9 copy.18
  227.7 0.0 copy-done
  227.7 0.9 copy.19
Async XLA Ops:
  222.0 3.9 %copy-start.2 = (bf16[512,768]{1,0:T(8,128)(2,1)S(1)}, bf16[512,768]{1,0:T(8,128)(2,1)}, u32[]{:S(2)}) copy-start(bf16[512,768]{1,0:T(8,128)(2,1)} %get-tuple-element.26) | copy-start | bytes 2359300
  223.3 3.5 %copy-start.1 = (bf16[512,768]{1,0:T(8,128)(2,1)S(1)}, bf16[512,768]{1,0:T(8,128)(2,1)}, u32[]{:S(2)}) copy-start(bf16[512,768]{1,0:T(8,128)(2,1)} %get-tuple-element.27) | copy-start | bytes 2359300
  225.9 1.8 copy-start

commit v3 on v2

--- a/solution.py
+++ b/solution.py
@@ -124,7 +124,7 @@
         table_out[0, 0:ranks, :] = jnp.where(hits, order, -1.0)
         weight = jnp.zeros((ranks, count), F32)
         for k in range(ids_ref.shape[0]):
-            weight = jnp.where(named[k], weight_ref[k : k + 1, :], weight)
+            weight = jnp.where(named[k], weight_ref[k : k + 1, :].astype(F32), weight)
         table_out[0, ranks : 2 * ranks, :] = weight
 
         rows[:, :, cap:, :] = jnp.zeros((steps, ranks, slot_rows - cap, width), BF16)
@@ -852,7 +852,7 @@
     for step in range(1, ranks):
         dots_from((me + step) % ranks).wait_recv()
     dots_in[me] = dots_ref[4 * c + z]
-    found = jnp.zeros(route_out.shape, F32)
+    found = jnp.zeros(ids_ref.shape, F32)
     slot = lax.broadcasted_iota(jnp.int32, (slot_rows, count), 0).astype(F32)
     for rank in range(ranks):
         hit = jnp.where(table_ref[0, rank : rank + 1, :] == slot, 1.0, 0.0)
@@ -861,7 +861,7 @@
             precision=lax.Precision.HIGHEST, preferred_element_type=F32,
         )[0:1, :]
         found = jnp.where(ids_ref[...] == rank, value, found)
-    route_out[...] = found / weight_ref[...]
+    route_out[...] = (found / weight_ref[...].astype(F32)).astype(BF16)
 
     def third(k, carry):
         columns = pl.ds(pl.multiple_of(k * narrow, 128), narrow)
@@ -932,11 +932,11 @@
     return pl.pallas_call(
         functools.partial(backward_kernel, cap),
         out_shape=(
-            jax.ShapeDtypeStruct((count, groups * width), BF16),
-            jax.ShapeDtypeStruct(ids_t.shape, F32),
-            jax.ShapeDtypeStruct((width, inner), BF16),
-            jax.ShapeDtypeStruct((width, inner), BF16),
-            jax.ShapeDtypeStruct((inner, width), BF16),
+            pltpu.VMEM((count, groups * width), BF16),
+            pltpu.VMEM(ids_t.shape, BF16),
+            pltpu.VMEM((width, inner), BF16),
+            pltpu.VMEM((width, inner), BF16),
+            pltpu.VMEM((inner, width), BF16),
         ),
         in_specs=[vmem, vmem, vmem, vmem, hbm, hbm, hbm, hbm, hbm],
         out_specs=(vmem,) * 5,
@@ -964,9 +964,29 @@
             dma((ranks,)), dma((ranks,)), dma((3, 2)), dma((3, 2)), dma((3, 2)), dma((3, 2)),
         ],
         compiler_params=pltpu.CompilerParams(
-            collective_id=1, has_side_effects=True, vmem_limit_bytes=67000000
+            collective_id=1, has_side_effects=True, vmem_limit_bytes=58000000
         ),
     )(ids_t, weight_t, table, dots, full, rows, hidden, delta, down)
+
+
+def hand_over_kernel(*refs):
+    ins, outs, sem = refs[0:5], refs[5:10], refs[10]
+    copies = [pltpu.make_async_copy(ins[i], outs[i], sem.at[i]) for i in range(5)]
+    for copy in copies:
+        copy.start()
+    for copy in copies:
+        copy.wait()
+
+
+def hand_over(*arrays):
+    return pl.pallas_call(
+        hand_over_kernel,
+        out_shape=tuple(jax.ShapeDtypeStruct(a.shape, a.dtype) for a in arrays),
+        in_specs=[pl.BlockSpec(memory_space=pltpu.VMEM)] * 5,
+        out_specs=(pl.BlockSpec(memory_space=pl.ANY),) * 5,
+        scratch_shapes=[pltpu.SemaphoreType.DMA((5,))],
+        compiler_params=pltpu.CompilerParams(vmem_limit_bytes=8000000),
+    )(*arrays)
 
 
 def swap(block, axis, distance):
@@ -1094,14 +1114,17 @@
 def on_device(tokens, out_grad, expert_ids, route_weight, w_gate, w_up, w_down):
     count = tokens.shape[0]
     cap = 3 * count * expert_ids.shape[1] // (2 * lax.axis_size("expert"))
-    ids_t, weight_t = expert_ids.T, route_weight.T.astype(F32)
+    ids_t, weight_t = expert_ids.T, route_weight.T
     full, rows, hidden, delta, dots, table, down = forward_call(
         ids_t, weight_t, tokens, out_grad, w_gate, w_up, w_down, cap
     )
     token_grad, route_grad, gate_grad, up_grad, down_grad = backward_call(
         ids_t, weight_t, table, dots, full, rows, hidden, delta, down, cap
     )
-    return token_grad, route_grad.T.astype(BF16), gate_grad[None], up_grad[None], down_grad[None]
+    token_grad, gate_grad, up_grad, down_grad, route_grad = hand_over(
+        token_grad, gate_grad, up_grad, down_grad, route_grad
+    )
+    return token_grad, route_grad.T, gate_grad[None], up_grad[None], down_grad[None]
 
 
 def solution(mesh):

time: 229 us -> 221 us (0.965)
  local copies, waits for them, and re-layouts: 5.24 us -> 0 us
  other arithmetic: 2.58 us -> 0 us
    unnamed x10 -> x0, local copies, waits for them, and re-layouts: 5.24 us -> none
    convert_element_type x2 -> x0, other arithmetic: 2.58 us -> none  [the longest x1 1.32 us: on_device(): route_grad.T.astype(BF16)]
    pallas_call x1 -> x2, Pallas kernels: 75.9 us -> 76 us  [the longest x1 74.1 us: backward_call(): pl.pallas_call(functools.partial(backward_kernel, cap), out_shape=(pltpu....]
where the time goes in v3:
time: 221 us
  Pallas kernels  220 us (100%)
    pallas_call x1, Pallas kernels, forward_call(): pl.pallas_call(functools.partial(forward_kernel, cap), out_shape=(jax.Sha...  144 us
    pallas_call x1, Pallas kernels, backward_call(): pl.pallas_call(functools.partial(backward_kernel, cap), out_shape=(pltpu....  74.1 us

profile of v3, /device:TPU:1, one launch (start us, length us, event | category | flops | bytes accessed | tf_op | source)
XLA Modules:
  0.0 221.0 jit_solution(15238178055454513209)
XLA Ops:
  0.6 144.2 %shard_map.110 = (bf16[2,4,512,768]{3,2,1,0:T(8,128)(2,1)}, bf16[5,8,128,512]{3,2,1,0:T(8,128)(2,1)}, bf16[8,128,768]{2,1,0:T(8,128)(2,1)}, bf16[2,8,128,768]{3,...) custom-call(s32[2,320]{1,0:T(2,128)} %bitcast.8, ...), custom_call_target="tpu_custom_call" | custom-call | tf_op jit(solution)/shard_map/pallas_call | solution.py:526
  144.8 74.1 %shard_map.111 = (bf16[320,2048]{1,0:T(8,128)(2,1)S(1)}, bf16[2,320]{1,0:T(2,128)(2,1)S(1)}, bf16[512,768]{1,0:T(8,128)(2,1)S(1)}, bf16[512,768]{1,0:T(8,128)(2,1)S(1)}, bf16[768,512]{1,0:T(8,128)(2,1)S(1)}) custom-call(s32[2,320]{1,0:T(2,128)} %bitcast.9, bf16[2,320]{1,0:T(2,128)(2,1)} %bitcast.11, f32[4,16,320]{2,1,0:T(8,128)} %get-tuple-element.22.table_ref, ...), custom_call_target="tpu_custom_call" | custom-call | tf_op jit(solution)/shard_map/pallas_call | solution.py:932
  218.9 1.9 shard_map.112

commit v4 on v3

--- a/solution.py
+++ b/solution.py
@@ -69,9 +69,9 @@
 def forward_kernel(
     cap,
     ids_ref, weight_ref, tokens_ref, grads_ref, wg_ref, wu_ref, wd_ref,
-    full_out, rows_out, hidden_out, delta_out, dots_out, table_out, down_out,
+    full_out, rows_out, hidden_hbm, delta_hbm, down_hbm, dots_out, table_out,
     raw, rows, stage_d, stage_e, full_gate, full_up, full_down, gate_val, up_val, hg_val, select,
-    down_part, down_relay, down_in,
+    down_part, down_relay, down_in, hidden_out, delta_out, down_out,
     load_sem, raw_ss, raw_rs, e_ss, e_rs, d_ss, d_rs, tab_ss, tab_rs,
     w_ls, wa_ss, wa_rs, wf_ss, wf_rs, out_sem, relay_ss, relay_rs, pair_ss, pair_rs,
 ):
@@ -89,18 +89,27 @@
     shards = (wg_ref, wu_ref, wd_ref)
 
     sub = width // groups
-    for k in range(groups):
-        pltpu.make_async_copy(
+
+    def load_x(k):
+        return pltpu.make_async_copy(
             tokens_ref.at[:, pl.ds(k * width, width)], raw.at[0, k], load_sem.at[k]
-        ).start()
-    for i in range(groups):
-        for owner in range(groups):
-            pltpu.make_async_copy(
-                grads_ref.at[:, pl.ds(owner * width + i * sub, sub)],
-                raw.at[0, groups + i, :, pl.ds(owner * sub, sub)], load_sem.at[groups + i],
-            ).start()
-    for w in range(3):
-        pltpu.make_async_copy(shards[w].at[0], fulls[w].at[g], w_ls.at[w]).start()
+        )
+
+    def load_rest():
+        for k in range(ahead, groups):
+            load_x(k).start()
+        for i in range(groups):
+            for owner in range(groups):
+                pltpu.make_async_copy(
+                    grads_ref.at[:, pl.ds(owner * width + i * sub, sub)],
+                    raw.at[0, groups + i, :, pl.ds(owner * sub, sub)], load_sem.at[groups + i],
+                ).start()
+        for w in range(3):
+            pltpu.make_async_copy(shards[w].at[0], fulls[w].at[g], w_ls.at[w]).start()
+
+    ahead = 3
+    for k in range(ahead):
+        load_x(k).start()
 
     def shard_to(w, way):
         device = (along_x, me) if way == 0 else (along_y, me)
@@ -201,7 +210,7 @@
             e_ss.at[k, 1 + which, 0], e_rs.at[k, 1 + which, core], chain.at(chain.z_mid, core),
         )
 
-    def landed(k):
+    def landed_near(k):
         @pl.when(is_mid)
         def _():
             mid_to_partner(k).wait_recv()
@@ -211,8 +220,17 @@
             end_to_partner(k).wait_recv()
             for core in range(2):
                 own_block_from(k, core).wait_recv()
+
+    def landed_far(k):
+        @pl.when(is_end)
+        def _():
+            for core in range(2):
                 for which in range(2):
                     far_block_from(k, core, which).wait_recv()
+
+    def landed(k):
+        landed_near(k)
+        landed_far(k)
 
     def load_wait(k):
         pltpu.make_async_copy(
@@ -224,8 +242,6 @@
     half_inner = hidden_out.shape[2] // 2
 
     def hidden_grad(q, carry):
-        landed(groups + q)
-
         def tile(t, carry):
             four = pl.ds(4 * t, 4)
             value = functools.reduce(jnp.add, [
@@ -248,6 +264,8 @@
 
         return lax.fori_loop(0, ranks // 4, tile, carry)
 
+    hidden_copy = pltpu.make_async_copy(hidden_out, hidden_hbm, out_sem.at[4])
+
     def block_of(tile):
         return pl.ds(tile * half_inner, half_inner)
 
@@ -295,8 +313,6 @@
             total = total + down_in[i, way].astype(F32)
         down_out[:, of_owner(i)] = total.astype(BF16)
 
-    ahead = 2
-
     def prologue():
         build_table()
         selectors(0)
@@ -328,6 +344,7 @@
     def _():
         table_send(2, 0, chain.z_far_mid).start()
 
+    load_rest()
     for w in range(1, 3):
         for way in range(2):
             shard_to(w, way).start()
@@ -361,6 +378,65 @@
                 own_to_end(k + ahead, 1).start()
 
             gather(1, k, chain.z_end, 2, 0)
+
+        @pl.when(is_end & (k < steps))
+        def _():
+            gather(0, k, z, 2, 0)
+            end_to_partner(k).start()
+
+        for w in range(3):
+            @pl.when(k == w + 2)
+            def _():
+                for way in range(2):
+                    shard_to(w, 1 - way).wait_recv()
+                    forward_half(w, way).start()
+
+        @pl.when(k == groups + 1)
+        def _():
+            for kk in range(groups):
+                landed(kk)
+            for w in range(2):
+                pltpu.make_async_copy(shards[w].at[0], fulls[w].at[g], w_ls.at[w]).wait()
+                for way in range(2):
+                    forward_half(w, way).wait_recv()
+
+        @pl.when((k == groups + 1) | (k == groups + 2))
+        def _():
+            def forward(p, carry):
+                pair = pl.ds(2 * p, 2)
+                shape = (2, slot_rows, gate_val.shape[2])
+                piece = [rows[kk, pair].reshape(2 * slot_rows, width) for kk in range(groups)]
+                gate = functools.reduce(jnp.add, [dot(piece[kk], full_gate[kk]) for kk in range(groups)])
+                up = functools.reduce(jnp.add, [dot(piece[kk], full_up[kk]) for kk in range(groups)])
+                gate_val[pair] = gate.reshape(shape)
+                up_val[pair] = up.reshape(shape)
+                hidden_out[pair] = (gate * jax.nn.sigmoid(gate) * up).astype(BF16).reshape(shape)
+                return carry
+
+            start = (k - groups - 1) * (ranks // 4)
+            lax.fori_loop(start, start + ranks // 4, forward, 0)
+
+        @pl.when(k == groups + 2)
+        def _():
+            pltpu.make_async_copy(shards[2].at[0], fulls[2].at[g], w_ls.at[2]).wait()
+            for way in range(2):
+                forward_half(2, way).wait_recv()
+
+        @pl.when(k >= groups + 2)
+        def _():
+            q = k - groups - 2
+
+            @pl.when(q >= 1)
+            def _():
+                down_pass(q - 1)
+
+            landed(groups + q)
+            down_make(q)
+            hidden_grad(q, 0)
+
+            @pl.when(q == 0)
+            def _():
+                hidden_copy.start()
 
         @pl.when(is_mid & (k >= 1))
         def _():
@@ -382,60 +458,6 @@
             far_to_end(j, 1, 1).start()
             mid_to_partner(j).start()
 
-        @pl.when(is_end & (k < steps))
-        def _():
-            gather(0, k, z, 2, 0)
-            end_to_partner(k).start()
-
-        for w in range(3):
-            @pl.when(k == w + 2)
-            def _():
-                for way in range(2):
-                    shard_to(w, 1 - way).wait_recv()
-                    forward_half(w, way).start()
-
-        @pl.when(k == groups + 1)
-        def _():
-            for kk in range(groups):
-                landed(kk)
-            for w in range(2):
-                pltpu.make_async_copy(shards[w].at[0], fulls[w].at[g], w_ls.at[w]).wait()
-                for way in range(2):
-                    forward_half(w, way).wait_recv()
-
-        @pl.when((k == groups + 1) | (k == groups + 2))
-        def _():
-            def forward(p, carry):
-                pair = pl.ds(2 * p, 2)
-                shape = (2, slot_rows, gate_val.shape[2])
-                piece = [rows[kk, pair].reshape(2 * slot_rows, width) for kk in range(groups)]
-                gate = functools.reduce(jnp.add, [dot(piece[kk], full_gate[kk]) for kk in range(groups)])
-                up = functools.reduce(jnp.add, [dot(piece[kk], full_up[kk]) for kk in range(groups)])
-                gate_val[pair] = gate.reshape(shape)
-                up_val[pair] = up.reshape(shape)
-                hidden_out[pair] = (gate * jax.nn.sigmoid(gate) * up).astype(BF16).reshape(shape)
-                return carry
-
-            start = (k - groups - 1) * (ranks // 4)
-            lax.fori_loop(start, start + ranks // 4, forward, 0)
-
-        @pl.when(k == groups + 2)
-        def _():
-            pltpu.make_async_copy(shards[2].at[0], fulls[2].at[g], w_ls.at[2]).wait()
-            for way in range(2):
-                forward_half(2, way).wait_recv()
-
-        @pl.when(k >= groups + 2)
-        def _():
-            q = k - groups - 2
-
-            @pl.when(q >= 1)
-            def _():
-                down_pass(q - 1)
-
-            hidden_grad(q, 0)
-            down_make(q)
-
         return carry
 
     lax.fori_loop(0, steps + 1, step, 0)
@@ -450,9 +472,6 @@
     first.start()
 
     down_pass(groups - 2)
-    hidden_grad(groups - 1, 0)
-    late = pltpu.make_async_copy(rows.at[steps - 1], rows_out.at[groups], out_sem.at[3])
-    late.start()
 
     def deltas(t, carry):
         gate, up, grad = gate_val[t], up_val[t], hg_val[t]
@@ -463,7 +482,37 @@
         dots_out[t] = jnp.broadcast_to(total, (total.shape[0], total.shape[0])).T[0:8, :]
         return carry
 
-    lax.fori_loop(0, ranks, deltas, 0)
+    late = pltpu.make_async_copy(rows.at[steps - 1], rows_out.at[groups], out_sem.at[3])
+
+    def delta_copy(side, core, half):
+        pair = pl.ds(4 * core + 2 * half, 2)
+        return pltpu.make_async_copy(
+            delta_out.at[:, pair], delta_hbm.at[:, pair], out_sem.at[6 + 2 * side + core]
+        )
+
+    for side, half in enumerate((chain.half, chain.far)):
+        if side == 0:
+            landed_near(steps - 1)
+        else:
+            landed_far(steps - 1)
+            late.start()
+
+        def last_rows(core, carry):
+            pair = pl.ds(4 * core + 2 * half, 2)
+            value = functools.reduce(jnp.add, [
+                dot(
+                    rows[steps - 1, pair, :, owner * sub : (owner + 1) * sub].reshape(2 * slot_rows, sub),
+                    full_down[owner, :, (groups - 1) * sub : groups * sub], 1, 1,
+                )
+                for owner in range(groups)
+            ])
+            hg_val[pair] += value.reshape(2, slot_rows, hg_val.shape[2])
+            for block in range(2):
+                deltas(4 * core + 2 * half + block, 0)
+            delta_copy(side, core, half).start()
+            return carry
+
+        lax.fori_loop(0, 2, last_rows, 0)
 
     for copy in outs:
         copy.wait()
@@ -478,6 +527,8 @@
         return carry
 
     lax.fori_loop(0, groups - 1, finish_down, 0)
+    down_copy = pltpu.make_async_copy(down_out, down_hbm, out_sem.at[5])
+    down_copy.start()
     for w in range(3):
         for way in range(2):
             shard_to(w, way).wait_send()
@@ -511,6 +562,12 @@
     def _():
         table_send(1, 0, chain.z_mid).wait_send()
         table_send(3, 1, chain.z_far_mid).wait_send()
+
+    hidden_copy.wait()
+    down_copy.wait()
+    for side, half in enumerate((chain.half, chain.far)):
+        for core in range(2):
+            delta_copy(side, core, half).wait()
 
 
 def forward_call(ids_t, weight_t, tokens, out_grad, w_gate, w_up, w_down, cap):
@@ -530,12 +587,12 @@
             jax.ShapeDtypeStruct((groups + 1, ranks, slot_rows, width), BF16),
             jax.ShapeDtypeStruct((ranks, slot_rows, inner), BF16),
             jax.ShapeDtypeStruct((2, ranks, slot_rows, inner), BF16),
+            jax.ShapeDtypeStruct((inner, width), BF16),
             jax.ShapeDtypeStruct((ranks, 8, slot_rows), F32),
             jax.ShapeDtypeStruct((4, 2 * ranks, count), F32),
-            jax.ShapeDtypeStruct((inner, width), BF16),
         ),
         in_specs=[vmem, vmem, hbm, hbm, hbm, hbm, hbm],
-        out_specs=(hbm, hbm, vmem, vmem, vmem, vmem, vmem),
+        out_specs=(hbm,) * 5 + (vmem,) * 2,
         scratch_shapes=[
             pltpu.VMEM((4, steps, count, width), BF16),
             pltpu.VMEM((steps, ranks, slot_rows, width), BF16),
@@ -551,9 +608,12 @@
             pltpu.VMEM((groups - 1, inner, width), BF16),
             pltpu.VMEM((groups - 1, 2, inner // 2, width // groups), BF16),
             pltpu.VMEM((groups - 1, 2, inner, width // groups), BF16),
+            pltpu.VMEM((ranks, slot_rows, inner), BF16),
+            pltpu.VMEM((2, ranks, slot_rows, inner), BF16),
+            pltpu.VMEM((inner, width), BF16),
             dma((steps,)), dma((2, steps)), dma((3, steps)), dma((steps, 3, 2)), dma((steps, 3, 2)),
             dma((steps,)), dma((steps,)), dma((2,)), dma((3,)),
-            dma((3,)), dma((3, 2)), dma((3, 2)), dma((3, 2)), dma((3, 2)), dma((4,)),
+            dma((3,)), dma((3, 2)), dma((3, 2)), dma((3, 2)), dma((3, 2)), dma((10,)),
             dma((groups - 1, 2)), dma((groups - 1, 2)), dma((groups - 1, 2)), dma((groups - 1, 2)),
         ],
         compiler_params=pltpu.CompilerParams(
@@ -763,6 +823,10 @@
             value = value.reshape(4, slot_rows, narrow)
             grads[k, pl.ds(4 * hc, 4)] = value
 
+            @pl.when(is_end)
+            def _():
+                far_home(k, hc).start()
+
             @pl.when(c == hc)
             def _():
                 comb[k, :, 0] = value
@@ -793,8 +857,6 @@
 
             @pl.when(is_end)
             def _():
-                for core in range(2):
-                    far_home(k, core).start()
                 end_to_partner(k).start()
 
         @pl.when(is_end & (k == subs - 1))
@@ -1115,7 +1177,7 @@
     count = tokens.shape[0]
     cap = 3 * count * expert_ids.shape[1] // (2 * lax.axis_size("expert"))
     ids_t, weight_t = expert_ids.T, route_weight.T
-    full, rows, hidden, delta, dots, table, down = forward_call(
+    full, rows, hidden, delta, down, dots, table = forward_call(
         ids_t, weight_t, tokens, out_grad, w_gate, w_up, w_down, cap
     )
     token_grad, route_grad, gate_grad, up_grad, down_grad = backward_call(

time: 221 us -> 215 us (0.973)
  Pallas kernels: 220 us -> 214 us
    pallas_call x1, Pallas kernels: 144 us -> 139 us  [forward_call(): pl.pallas_call(functools.partial(forward_kernel, cap), out_shape=(jax.Sha...]
where the time goes in v4:
time: 215 us
  Pallas kernels  214 us (100%)
    pallas_call x1, Pallas kernels, forward_call(): pl.pallas_call(functools.partial(forward_kernel, cap), out_shape=(jax.Sha...  139 us
    pallas_call x1, Pallas kernels, backward_call(): pl.pallas_call(functools.partial(backward_kernel, cap), out_shape=(pltpu....  73.1 us

profile of v4, /device:TPU:1, one launch (start us, length us, event | category | flops | bytes accessed | tf_op | source)
XLA Modules:
  0.0 214.6 jit_solution(11570389684405602764)
XLA Ops:
  0.6 138.8 %shard_map.110 = (bf16[2,4,512,768]{3,2,1,0:T(8,128)(2,1)}, bf16[5,8,128,512]{3,2,1,0:T(8,128)(2,1)}, bf16[8,128,768]{2,1,0:T(8,128)(2,1)}, bf16[2,8,128,768]{3,...) custom-call(s32[2,320]{1,0:T(2,128)} %bitcast.8, ...), custom_call_target="tpu_custom_call" | custom-call | tf_op jit(solution)/shard_map/pallas_call | solution.py:583
  139.5 73.1 %shard_map.111 = (bf16[320,2048]{1,0:T(8,128)(2,1)S(1)}, bf16[2,320]{1,0:T(2,128)(2,1)S(1)}, bf16[512,768]{1,0:T(8,128)(2,1)S(1)}, bf16[512,768]{1,0:T(8,128)(2,1)S(1)}, bf16[768,512]{1,0:T(8,128)(2,1)S(1)}) custom-call(s32[2,320]{1,0:T(2,128)} %bitcast.9, bf16[2,320]{1,0:T(2,128)(2,1)} %bitcast.11, f32[4,16,320]{2,1,0:T(8,128)} %get-tuple-element.22.table_ref, ...), custom_call_target="tpu_custom_call" | custom-call | tf_op jit(solution)/shard_map/pallas_call | solution.py:994
  212.6 1.9 shard_map.112

commit v5 on v4

--- a/solution.py
+++ b/solution.py
@@ -711,18 +711,18 @@
             d_ss.at[k], d_rs.at[k], chain.at(z, 1 - c),
         )
 
-    def far_home(k, core):
-        return send(
-            grads.at[k, pl.ds(4 * core + 2 * chain.far, 2), real],
-            comb.at[k, pl.ds(2 * chain.far, 2), 2 + c, real],
-            far_ss.at[k, core], far_rs.at[k, c], chain.at(chain.z_mid, core),
-        )
-
-    def far_from(k, core):
-        return send(
-            grads.at[k, pl.ds(4 * core + 2 * chain.far, 2), real],
-            comb.at[k, pl.ds(2 * chain.far, 2), 2 + core, real],
-            far_ss.at[k, core], far_rs.at[k, core], chain.at(chain.z_end, core),
+    homes = (chain.z_far_mid, chain.z_far_end)
+
+    def far_home(k, core, home):
+        return send(
+            grads.at[k, 4 * core + homes[home], real], comb.at[k, homes[home], 2 + c, real],
+            far_ss.at[k, core, home], far_rs.at[k, c, home], chain.at(chain.z_mid, core),
+        )
+
+    def far_from(k, core, home):
+        return send(
+            grads.at[k, 4 * core + homes[home], real], comb.at[k, homes[home], 2 + core, real],
+            far_ss.at[k, core, home], far_rs.at[k, core, home], chain.at(chain.z_end, core),
         )
 
     def near_home(k, core):
@@ -825,7 +825,7 @@
 
             @pl.when(is_end)
             def _():
-                far_home(k, hc).start()
+                far_home(k, hc, 1).start()
 
             @pl.when(c == hc)
             def _():
@@ -857,6 +857,8 @@
 
             @pl.when(is_end)
             def _():
+                for core in range(2):
+                    far_home(k, core, 0).start()
                 end_to_partner(k).start()
 
         @pl.when(is_end & (k == subs - 1))
@@ -884,9 +886,11 @@
             j = k - 1
             to_partner(j).wait_recv()
             for core in range(2):
-                far_from(j, core).wait_recv()
+                far_from(j, core, 1).wait_recv()
             gf_send[j, 1] = summed(j, chain.z_far_end, 4).astype(BF16)
             sums_across(j, 1).start()
+            for core in range(2):
+                far_from(j, core, 0).wait_recv()
             gf_send[j, 0] = summed(j, chain.z_far_mid, 4).astype(BF16)
             sums_across(j, 0).start()
 
@@ -936,6 +940,10 @@
         def _():
             finish(2)
 
+        @pl.when(k == subs - 1)
+        def _():
+            finish(1)
+
         @pl.when(is_mid)
         def _():
             sums_across(k, 0).wait_recv()
@@ -953,7 +961,6 @@
 
     lax.fori_loop(0, subs, third, 0)
 
-    finish(1)
     for w in range(3):
         for way in range(2):
             relay_to(w, way).wait_send()
@@ -972,7 +979,8 @@
         @pl.when(is_end)
         def _():
             for core in range(2):
-                far_home(k, core).wait_send()
+                for home in range(2):
+                    far_home(k, core, home).wait_send()
                 near_home(k, core).wait_send()
             end_to_partner(k).wait_send()
 
@@ -1021,7 +1029,7 @@
             pltpu.VMEM((2, 2, width, inner), BF16),
             pltpu.VMEM((2, inner, width // groups), BF16),
             pltpu.VMEM(dots.shape, F32),
-            dma((12,)), dma((subs,)), dma((subs,)), dma((subs, 2)), dma((subs, 2)),
+            dma((12,)), dma((subs,)), dma((subs,)), dma((subs, 2, 2)), dma((subs, 2, 2)),
             dma((subs, 2)), dma((subs, 2)), dma((subs, 2)), dma((subs, 2)), dma((subs,)), dma((subs,)),
             dma((ranks,)), dma((ranks,)), dma((3, 2)), dma((3, 2)), dma((3, 2)), dma((3, 2)),
         ],

time: 215 us -> 214 us (level)
  Pallas kernels: 214 us -> 211 us
    pallas_call x1, Pallas kernels: 73.1 us -> 70.5 us  [backward_call(): pl.pallas_call(functools.partial(backward_kernel, cap), out_shape=(pltpu....]
where the time goes in v5:
time: 214 us; the launch traced here: 212 us
  Pallas kernels  211 us (99%)
    pallas_call x1, Pallas kernels, forward_call(): pl.pallas_call(functools.partial(forward_kernel, cap), out_shape=(jax.Sha...  139 us
    pallas_call x1, Pallas kernels, backward_call(): pl.pallas_call(functools.partial(backward_kernel, cap), out_shape=(pltpu....  70.5 us

profile of v5, /device:TPU:1, one launch (start us, length us, event | category | flops | bytes accessed | tf_op | source)
XLA Modules:
  0.0 212.0 jit_solution(4128531353026361773)
XLA Ops:
  0.6 138.8 %shard_map.110 = (bf16[2,4,512,768]{3,2,1,0:T(8,128)(2,1)}, bf16[5,8,128,512]{3,2,1,0:T(8,128)(2,1)}, bf16[8,128,768]{2,1,0:T(8,128)(2,1)}, bf16[2,8,128,768]{3,...) custom-call(s32[2,320]{1,0:T(2,128)} %bitcast.8, ...), custom_call_target="tpu_custom_call" | custom-call | tf_op jit(solution)/shard_map/pallas_call | solution.py:583
  139.5 70.5 %shard_map.111 = (bf16[320,2048]{1,0:T(8,128)(2,1)S(1)}, bf16[2,320]{1,0:T(2,128)(2,1)S(1)}, bf16[512,768]{1,0:T(8,128)(2,1)S(1)}, bf16[512,768]{1,0:T(8,128)(2,1)S(1)}, bf16[768,512]{1,0:T(8,128)(2,1)S(1)}) custom-call(s32[2,320]{1,0:T(2,128)} %bitcast.9, bf16[2,320]{1,0:T(2,128)(2,1)} %bitcast.11, f32[4,16,320]{2,1,0:T(8,128)} %get-tuple-element.22.table_ref, ...), custom_call_target="tpu_custom_call" | custom-call | tf_op jit(solution)/shard_map/pallas_call | solution.py:1002
  210.0 1.9 shard_map.112
